TPU v7x, 128 devices: a whole 4x4x4 slice. The times are simulated.
128 devices in a mesh: node: 32 (over y, z, core), feat: 4 (over x).
Axes of the slice: x: 4, y: 4, z: 4, core: 2. Of those that a mesh axis runs over, the one named last changes fastest.
Arguments:
- memory: float32 [32768, 172], P('node')
- last_update: int32 [32768], P('node'), may hold values from 6000 to 9999
- ev_time: int32 [65536], P(('node', 'feat')), may hold values from 10000 to 11999
- nbr_gap: int32 [65536, 10], P(('node', 'feat')), may hold values from 1 to 1999
- slot_rows: int32 [128, 1536], P(('node', 'feat')), may hold values from -1 to 1023, as said below
- slot_ref: int32 [65536, 12], P(('node', 'feat')), may hold values from 0 to 1535, as said below
- edge_feat: bfloat16 [65536, 256], P('node', 'feat'), may hold values from -6 to 6
- frequency: float32 [100], replicated, may hold values from 0.001 to 0.1
- phase_shift: float32 [100], replicated, may hold values from -3.140625 to 3.140625
- w_query: bfloat16 [272, 272], replicated, may hold values from -0.375 to 0.375
- w_key: bfloat16 [272, 272], replicated, may hold values from -0.375 to 0.375
- w_value: bfloat16 [272, 272], replicated, may hold values from -0.375 to 0.375
- w_merge: bfloat16 [444, 172], replicated, may hold values from -0.25 to 0.25
- b_merge: float32 [172], replicated, may hold values from -3 to 3
- w_out: bfloat16 [172, 172], replicated, may hold values from -0.4375 to 0.4375
- b_out: float32 [172], replicated, may hold values from -3 to 3
- w_input: float32 [3, 700, 172], P(None, None, 'feat'), may hold values from -0.21875 to 0.21875
- w_hidden: float32 [3, 172, 172], P(None, None, 'feat'), may hold values from -0.4375 to 0.4375
- gru_bias: float32 [4, 172], P(None, 'feat'), may hold values from -3 to 3
Outputs:
- embedding: bfloat16 [65536, 172], P(('node', 'feat'))
- new_memory: float32 [32768, 172], P('node', 'feat')
Inputs may be any that keep to these rules, and one draw needn't show every extreme that they name: `slot_rows`: row r lists the nodes read by events r * 512 to (r + 1) * 512 - 1: slot s asks owner s // 48 (an index along node) for one of its local rows, or holds -1. Within one owner's 48 slots the live ones come first and name distinct rows; every row has 1024 live slots. `slot_ref`: entries of event e name live slots of row e // 512 of slot_rows; every live slot is named by some event of its block.
All inputs are finite; a program needn't handle non-finite values.
Results may differ from a plain program's by a relative error of at most 0.01.
Values may be sent and summed in bfloat16 or wider, within the bound.
A program may use at most 128 MiB of HBM per device.

v0:
```python
import math

import jax
import jax.numpy as jnp
from jax import lax
from jax.sharding import PartitionSpec as P

HEADS = 2


def sent_together(arrays, axis, split_dim, concat_dim, along):
    columns = [a.reshape(*a.shape[:along], -1) for a in arrays]
    both = jnp.concatenate(columns, axis=along)
    out, at, done = (
        lax.all_to_all(both, axis, split_axis=split_dim, concat_axis=concat_dim, tiled=True),
        0,
        [],
    )
    for a, column in zip(arrays, columns):
        slab = out[..., at : at + column.shape[along]]
        done.append(slab.reshape(*slab.shape[:along], *a.shape[along:]))
        at += column.shape[along]
    return tuple(done)


def laid_out(pieces, dim):
    shape = list(pieces.shape[1:])
    shape[dim] *= pieces.shape[0]
    return jnp.moveaxis(pieces, 0, dim).reshape(shape)


def from_everyone(array, axis):
    copies = jnp.broadcast_to(array, (lax.axis_size(axis), *array.shape))
    return lax.all_to_all(copies, axis, split_axis=0, concat_axis=0, tiled=True)


def gather_directly(array, axis, dim):
    return laid_out(from_everyone(array, axis), dim)


def cut_along(array, dim, length):
    shape = array.shape
    pieces = array.reshape(*shape[:dim], length, shape[dim] // length, *shape[dim + 1 :])
    return jnp.moveaxis(pieces, dim, 0)


def summed_on_arrival(array, axis, dim):
    pieces = cut_along(array, dim, lax.axis_size(axis))
    arrived = lax.all_to_all(pieces, axis, split_axis=0, concat_axis=0, tiled=True)
    return arrived.astype(jnp.float32).sum(axis=0)


def time_code(gap_vals, frequency, phase_shift):
    return jnp.cos(gap_vals[..., None] * frequency + phase_shift)


def embed_events(
    source,
    neighbors,
    gap_vals,
    frequency,
    phase_shift,
    w_query,
    w_key,
    w_value,
    w_merge,
    b_merge,
    w_out,
    b_out,
):
    event_count = source.shape[0]
    nbr_count = neighbors.shape[1]
    att_width = w_query.shape[0]
    head_size = att_width // HEADS
    still_code = jnp.broadcast_to(jnp.cos(phase_shift), (event_count, phase_shift.shape[0]))
    query_in = jnp.concatenate([source, still_code], 1).astype(jnp.bfloat16)
    key_in = jnp.concatenate([neighbors, time_code(gap_vals, frequency, phase_shift)], 2).astype(
        jnp.bfloat16
    )
    key_in = key_in.reshape(event_count * nbr_count, att_width)
    queries = jnp.dot(query_in, w_query, preferred_element_type=jnp.float32).reshape(
        event_count, HEADS, head_size
    )
    key_vecs = jnp.dot(key_in, w_key, preferred_element_type=jnp.float32).reshape(
        event_count, nbr_count, HEADS, head_size
    )
    values = jnp.dot(key_in, w_value, preferred_element_type=jnp.float32).reshape(
        event_count, nbr_count, HEADS, head_size
    )
    scores = jnp.einsum("ehd,ekhd->ehk", queries, key_vecs) / math.sqrt(head_size)
    weights = jax.nn.softmax(scores, axis=2)
    attended = jnp.einsum("ehk,ekhd->ehd", weights, values).reshape(event_count, att_width)
    merged = jnp.concatenate([attended, source], 1).astype(jnp.bfloat16)
    hidden = jax.nn.relu(
        jnp.dot(merged, w_merge, preferred_element_type=jnp.float32) + b_merge
    ).astype(jnp.bfloat16)
    return (jnp.dot(hidden, w_out, preferred_element_type=jnp.float32) + b_out).astype(jnp.bfloat16)


def build_messages(
    source, target, stamp_src, stamp_dst, ev_time, edge_rows, frequency, phase_shift
):
    code_src = time_code(ev_time - stamp_src, frequency, phase_shift)
    code_dst = time_code(ev_time - stamp_dst, frequency, phase_shift)
    wide_edges = edge_rows.astype(jnp.float32)
    to_source = jnp.concatenate([source, target, code_src, wide_edges], 1)
    to_target = jnp.concatenate([target, source, code_dst, wide_edges], 1)
    return jnp.concatenate([to_source, to_target], 0)


def gru_update(inputs, previous, own_cols, w_hidden, gru_bias):
    recurrent = jnp.einsum("rn,gnm->grm", previous, w_hidden)
    reset_gate = jax.nn.sigmoid(inputs[0] + recurrent[0] + gru_bias[0])
    update_gate = jax.nn.sigmoid(inputs[1] + recurrent[1] + gru_bias[1])
    candidate = jnp.tanh(inputs[2] + gru_bias[2] + reset_gate * (recurrent[2] + gru_bias[3]))
    return (1.0 - update_gate) * candidate + update_gate * own_cols


def take_rows(lookup, source_table, source_stamps):
    safe_ids = jnp.maximum(lookup, 0)
    picked = jnp.take(source_table, safe_ids, axis=0)
    found_stamps = jnp.take(source_stamps, safe_ids, axis=0).astype(jnp.float32)
    return (picked, found_stamps)


def sum_rows(lookup, source_vals, weights, total):
    sums = jax.ops.segment_sum(source_vals, lookup, num_segments=total)
    hit_counts = jax.ops.segment_sum(weights, lookup, num_segments=total)
    return (sums, hit_counts)


def per_device(
    memory,
    last_update,
    ev_time,
    nbr_gap,
    slot_rows,
    slot_ref,
    edge_feat,
    frequency,
    phase_shift,
    w_query,
    w_key,
    w_value,
    w_merge,
    b_merge,
    w_out,
    b_out,
    w_input,
    w_hidden,
    gru_bias,
):
    node_count = lax.axis_size("node")
    row_count = memory.shape[0]
    mem_width = memory.shape[1]
    slot_count = slot_rows.shape[1]
    per_owner = slot_count // node_count
    requested = lax.all_to_all(
        slot_rows.reshape(node_count, per_owner), "node", split_axis=0, concat_axis=0, tiled=True
    ).reshape(slot_count)
    found_rows, found_stamps = take_rows(requested, memory, last_update)
    fetched, fetched_stamps = sent_together(
        (
            found_rows.reshape(node_count, per_owner, mem_width),
            found_stamps.reshape(node_count, per_owner),
        ),
        "node",
        0,
        0,
        2,
    )
    fetched = fetched.reshape(slot_count, mem_width)
    fetched_stamps = fetched_stamps.reshape(slot_count)
    edge_rows = lax.all_to_all(edge_feat, "feat", split_axis=0, concat_axis=1, tiled=True)
    picked = jnp.take(fetched, slot_ref, axis=0)
    stamps = jnp.take(fetched_stamps, slot_ref[:, :2], axis=0)
    embedding = embed_events(
        picked[:, 0],
        picked[:, 2:],
        nbr_gap.astype(jnp.float32),
        frequency,
        phase_shift,
        w_query,
        w_key,
        w_value,
        w_merge,
        b_merge,
        w_out,
        b_out,
    )
    message_rows = build_messages(
        picked[:, 0],
        picked[:, 1],
        stamps[:, 0],
        stamps[:, 1],
        ev_time,
        edge_rows,
        frequency,
        phase_shift,
    )
    endpoints = jnp.concatenate([slot_ref[:, 0], slot_ref[:, 1]])
    unit_weights = jnp.ones(endpoints.shape, jnp.float32)
    width_cols = w_hidden.shape[2]
    own_cols = lax.dynamic_slice_in_dim(memory, lax.axis_index("feat") * width_cols, width_cols, 1)
    full_input = gather_directly(w_input, "feat", 2)
    projected = jnp.einsum("en,gnm->egm", message_rows, full_input).reshape(
        message_rows.shape[0], -1
    )
    slot_sums, slot_hits = sum_rows(endpoints, projected, unit_weights, slot_count)
    back_sums, back_hits = tuple(
        (
            part.astype(jnp.float32)
            for part in sent_together(
                (
                    slot_sums.reshape(node_count, per_owner, -1).astype(jnp.bfloat16),
                    slot_hits.reshape(node_count, per_owner).astype(jnp.bfloat16),
                ),
                "node",
                0,
                0,
                2,
            )
        )
    )
    node_sums, node_hits = sum_rows(
        requested, back_sums.reshape(slot_count, -1), back_hits.reshape(slot_count), row_count
    )
    spread = jnp.broadcast_to(node_hits[:, None, None], (row_count, 1, lax.axis_size("feat")))
    shares, hit_totals = (
        summed_on_arrival(node_sums.reshape(row_count, 3, -1).astype(jnp.bfloat16), "feat", 2),
        summed_on_arrival(spread.astype(jnp.bfloat16), "feat", 2),
    )
    touched = hit_totals[:, 0, 0]
    inputs = jnp.transpose(shares, (1, 0, 2)) / jnp.maximum(touched, 1.0)[None, :, None]
    renewed = gru_update(inputs, memory, own_cols, w_hidden, gru_bias)
    new_memory = jnp.where((touched > 0.0)[:, None], renewed, own_cols)
    return (embedding, new_memory)


def solution(mesh):
    return jax.shard_map(
        per_device,
        mesh=mesh,
        in_specs=(
            P("node", None),
            P("node"),
            P(("node", "feat")),
            P(("node", "feat"), None),
            P(("node", "feat"), None),
            P(("node", "feat"), None),
            P("node", "feat"),
            P(),
            P(),
            P(),
            P(),
            P(),
            P(),
            P(),
            P(),
            P(),
            P(None, None, "feat"),
            P(None, None, "feat"),
            P(None, "feat"),
        ),
        out_specs=(P(("node", "feat"), None), P("node", "feat")),
        check_vma=False,
    )
```

profile of v0, /device:TPU:1, one launch (start us, length us, event | category | flops | bytes accessed | tf_op | source)
XLA Modules:
  0.0 233.5 jit_solution(8303584950062793154)
XLA Ops:
  0.7 0.8 reduce.3
  2.2 9.6 %all-to-all-start = ((s32[32,1,48]{2,1,0:T(1,128)}), s32[32,1,48]{2,1,0:T(1,128)S(1)}, u32[]{:S(2)}, u32[]{:S(2)}) async-start(s32[32,1,48]{2,1,0:T(1,128)} %all_to_all.31), calls=%async_computation | async-start | bytes 32768 | tf_op jit(solution)/shard_map/all_to_all | solution.py:158
  12.5 0.8 compare_select_fusion.1
  13.2 0.8 fusion.71
  15.0 1.4 copy.79
  17.7 1.0 all-to-all-done
  18.7 1.0 broadcast_in_dim.93
  19.6 4.2 %all-to-all-start.3 = ((bf16[4,3,700,43]{2,3,1,0:T(8,128)(2,1)}), bf16[4,3,700,43]{2,3,1,0:T(8,128)(2,1)}, u32[]{:S(2)}, u32[]{:S(2)}) async-start(bf16[4,3,700,43]{2,3,1,0:T(8,128)(2,1)} %broadcast_in_dim.93), calls=%async_computation.3 | async-start | bytes 1769472 | tf_op jit(solution)/shard_map/all_to_all | solution.py:34
  24.0 5.9 %gather_fusion.1 = s32[1536]{0:T(1024)S(1)} fusion(s32[1024]{0:T(1024)S(1)} %copy-done.1, s32[2048]{0:T(1024)S(1)} %pad_clamp_fusion), kind=kCustom, calls=%fused_computation.1 | custom fusion | bytes 18432 | tf_op jit(solution)/shard_map/jit(_take)/gather | solution.py:122
  29.9 3.7 %gather_fusion = f32[1536,172]{1,0:T(8,128)S(1)} fusion(f32[1024,172]{1,0:T(8,128)S(1)} %copy.79, s32[2048]{0:T(1024)S(1)} %pad_clamp_fusion), kind=kCustom, calls=%fused_computation | custom fusion | bytes 2119680 | tf_op jit(solution)/shard_map/jit(_take)/gather | solution.py:121
  34.2 1.5 pad_maximum_fusion.1
  35.7 0.9 all-to-all-done.3
  36.6 7.6 %all-to-all-start.1 = ((f32[32,48,173]{2,1,0:T(8,128)}), f32[32,48,173]{2,1,0:T(8,128)S(1)}, u32[]{:S(2)}, u32[]{:S(2)}) async-start(f32[32,48,173]{2,1,0:T(8,128)} %pad_maximum_fusion.1), calls=%async_computation.1 | async-start | bytes 3145728 | tf_op jit(solution)/shard_map/all_to_all | solution.py:15
  44.2 6.1 %scatter_custom_fusion.1 = f32[1536]{0:T(1024)S(1)} fusion(s32[1024]{0:T(1024)S(1)} %pad_add_fusion, f32[1024]{0:T(1024)S(1)} %broadcast.97, f32[]{:T(128)} %constant.56.clone.1), kind=kCustom, calls=%fused_computation.104 | custom fusion | flops 1024 | bytes 6148 | tf_op jit(solution)/shard_map/scatter-add | solution.py:128
  50.3 1.5 convert_element_type.107
  51.8 0.8 copy.83
  52.7 0.8 copy.84
  53.6 7.9 %cosine_convert_fusion = bf16[512,10,100]{0,2,1:T(8,128)(2,1)} fusion(f32[100]{0:T(128)S(1)} %copy-done.26, f32[100]{0:T(128)S(1)} %copy-done.27, f32[512,10]{0,1:T(8,128)S(1)} %convert_element_type.86), kind=kLoop, calls=%fused_computation.32 | loop fusion | flops 1536000 | bytes 1045280 | tf_op jit(solution)/shard_map/convert.8
  61.5 1.2 copy.87
  62.7 1.3 reshape.183
  64.0 2.2 dot_general.51
  66.9 3.6 %all-to-all-start.2 = ((bf16[4,512,64]{1,2,0:T(8,128)(2,1)}), bf16[4,512,64]{1,2,0:T(8,128)(2,1)S(1)}, u32[]{:S(2)}, u32[]{:S(2)}) async-start(bf16[4,512,64]{1,2,0:T(8,128)(2,1)} %bitcast.139), calls=%async_computation.2 | async-start | bytes 524288 | tf_op jit(solution)/shard_map/all_to_all | solution.py:174
  71.1 6.2 %gather_fusion.3 = f32[1024]{0:T(1024)S(1)} fusion(f32[1536]{0:T(1024)S(1)} %reshape_reshape.4, s32[1024]{0:T(1024)S(1)} %broadcast_clamp_fusion.1), kind=kCustom, calls=%fused_computation.3 | custom fusion | bytes 12288 | tf_op jit(solution)/shard_map/jit(_take)/gather | solution.py:176
  77.9 25.0 %gather_fusion.2 = bf16[6144,172]{1,0:T(8,128)(2,1)} fusion(bf16[1536,172]{1,0:T(8,128)(2,1)S(1)} %bitcast.141, s32[6144]{0:T(1024)S(1)} %broadcast_clamp_fusion), kind=kCustom, calls=%fused_computation.2 | custom fusion | bytes 4251648 | tf_op jit(solution)/shard_map/jit(_take)/gather | solution.py:175
  102.9 6.6 %reshape.207 = bf16[512,12,172]{2,1,0:T(8,128)(2,1)} reshape(bf16[6144,172]{1,0:T(8,128)(2,1)} %gather_fusion.2) | data formatting | bytes 4227072 | tf_op jit(solution)/shard_map/jit(_take)/gather | solution.py:175
  109.5 7.5 %copy.82 = bf16[512,12,172]{0,2,1:T(8,128)(2,1)S(1)} copy(bf16[512,12,172]{2,1,0:T(8,128)(2,1)} %reshape.207) | data formatting | bytes 4227072 | tf_op jit(solution)/shard_map/jit(_take)/gather | solution.py:175
  117.5 1.4 copy-done.3
  119.0 1.5 add_cosine_fusion.1
  120.5 7.6 %fusion.2 = f32[1024,516]{1,0:T(8,128)} fusion(bf16[516,700]{1,0:T(8,128)(2,1)S(1)} %copy-done.11, bf16[512,256]{0,1:T(8,128)(2,1)S(1)} %bitcast.149, bf16[512,100]{0,1:T(8,128)(2,1)S(1)} %get-tuple-element.18, bf16[512,172]{0,1:T(8,128)(2,1)S(1)} %get-tuple-element.7, bf16[512,172]{0,1:T(8,128)(2,1)S(1)} %get-tuple-element.6, ...), kind=kOutput, calls=%fused_computation.13 | convolution fusion | flops 751206400 | bytes 3655136 | tf_op jit(solution)/shard_map/en,gnm->egm/dot_general | solution.py:206
  128.2 9.9 %scatter_custom_fusion = f32[1536,516]{1,0:T(8,128)} fusion(s32[1024]{0:T(1024)S(1)} %pad_add_fusion, f32[1024,516]{1,0:T(8,128)} %fusion.2, f32[]{:T(128)} %constant.56.clone.1), kind=kCustom, calls=%fused_computation.34 | custom fusion | flops 528384 | bytes 3170816 | tf_op jit(solution)/shard_map/scatter-add | solution.py:127
  138.1 2.4 %convert_element_type.93 = bf16[1536,516]{1,0:T(8,128)(2,1)S(1)} convert(f32[1536,516]{1,0:T(8,128)} %scatter_custom_fusion) | non-fusion elementwise | flops 792576 | bytes 4755456 | tf_op jit(solution)/shard_map/convert_element_type | solution.py:215
  140.5 1.6 pad_maximum_fusion
  142.1 7.0 %all-to-all-start.4 = ((bf16[32,48,517]{2,1,0:T(8,128)(2,1)}), bf16[32,48,517]{2,1,0:T(8,128)(2,1)S(1)}, u32[]{:S(2)}, u32[]{:S(2)}) async-start(bf16[32,48,517]{2,1,0:T(8,128)(2,1)} %pad_maximum_fusion), calls=%async_computation.4 | async-start | bytes 3932160 | tf_op jit(solution)/shard_map/all_to_all | solution.py:15
  149.7 1.0 convolution_bitcast_fusion
  152.0 1.7 slice.180
  154.2 1.7 multiply_reduce_fusion.1
  156.0 20.0 %all-to-all-done.4 = bf16[32,48,517]{2,1,0:T(8,128)(2,1)S(1)} async-done(((bf16[32,48,517]{2,1,0:T(8,128)(2,1)}), bf16[32,48,517]{2,1,0:T(8,128)(2,1)S(1)}, u32[]{:S(2)}, u32[]{:S(2)}) %all-to-all-start.4) | async-done | bytes 1588256 | tf_op jit(solution)/shard_map/all_to_all | solution.py:15
  176.5 9.9 %scatter_custom_fusion.2 = f32[1024]{0:T(1024)S(1)} fusion(s32[1536]{0:T(1024)S(1)} %reshape.240, f32[1536]{0:T(1024)S(1)} %reshape.242, f32[]{:T(128)} %constant.56.clone.1), kind=kCustom, calls=%fused_computation.111 | custom fusion | flops 1536 | bytes 4100 | tf_op jit(solution)/shard_map/scatter-add | solution.py:128
  188.3 4.3 %all-to-all-start.5 = ((bf16[4,2,512]{2,1,0:T(2,128)(2,1)}), bf16[4,2,512]{2,1,0:T(2,128)(2,1)}, u32[]{:S(2)}, u32[]{:S(2)}) async-start(bf16[4,2,512]{2,1,0:T(2,128)(2,1)} %reshape.296), calls=%async_computation.5 | async-start | bytes 16384 | tf_op jit(solution)/shard_map/all_to_all | solution.py:49
  192.6 4.3 %multiply_reduce_fusion = bf16[512,2,136]{0,2,1:T(8,128)(2,1)} fusion(f32[512,2,10]{0,1,2:T(2,128)S(1)} %broadcast_divide_fusion, bf16[2,136,272,1]{2,1,0,3:T(8,128)(2,1)S(1)} %bitcast.152, bf16[512,10,100]{0,2,1:T(8,128)(2,1)} %cosine_convert_fusion, bf16[512,10,172]{0,2,1:T(8,128)(2,1)} %copy-done.8), kind=kOutput, calls=%fused_computation.8 | convolution fusion | flops 765812736 | bytes 3252736 | tf_op jit(solution)/shard_map/dot_general | solution.py:87
  196.9 11.8 %scatter_custom_fusion.3 = f32[1024,516]{1,0:T(8,128)S(1)} fusion(s32[1536]{0:T(1024)} %copy-done.25, bf16[1536,516]{1,0:T(8,128)(2,1)} %bitcast.142, f32[]{:T(128)} %constant.56.clone.1), kind=kCustom, calls=%fused_computation.10 | custom fusion | flops 1585152 | bytes 4080128 | tf_op jit(solution)/shard_map/scatter-add | solution.py:127
  208.7 1.5 copy.90
  210.2 1.5 convert_element_type.102
  211.8 1.2 copy.91
  212.9 4.2 %all-to-all-start.6 = ((bf16[4,1024,3,43]{1,3,2,0:T(8,128)(2,1)}), bf16[4,1024,3,43]{1,3,2,0:T(8,128)(2,1)S(1)}, u32[]{:S(2)}, u32[]{:S(2)}) async-start(bf16[4,1024,3,43]{1,3,2,0:T(8,128)(2,1)} %copy.91), calls=%async_computation.6 | async-start | bytes 2359296 | tf_op jit(solution)/shard_map/all_to_all | solution.py:49
  217.3 1.1 fusion.22
  219.2 13.0 %all-to-all-done.6 = bf16[4,1024,3,43]{1,3,2,0:T(8,128)(2,1)S(1)} async-done(((bf16[4,1024,3,43]{1,3,2,0:T(8,128)(2,1)}), bf16[4,1024,3,43]{1,3,2,0:T(8,128)(2,1)S(1)}, u32[]{:S(2)}, u32[]{:S(2)}) %all-to-all-start.6) | async-done | bytes 1056800 | tf_op jit(solution)/shard_map/all_to_all | solution.py:49
  232.5 1.0 fusion.40
  (134 shorter events, 12.8 us)
Async XLA Ops:
  0.6 153.1 %copy-start = (bf16[272,272]{1,0:T(8,128)(2,1)S(1)}, bf16[272,272]{1,0:T(8,128)(2,1)}, u32[]{:S(2)}) copy-start(bf16[272,272]{1,0:T(8,128)(2,1)} %param.28) | copy-start | bytes 443908
  0.6 16.3 %copy-start.15 = (bf16[2048,64]{0,1:T(8,128)(2,1)S(1)}, bf16[2048,64]{0,1:T(8,128)(2,1)}, u32[]{:S(2)}) copy-start(bf16[2048,64]{0,1:T(8,128)(2,1)} %param.25) | copy-start | bytes 786436
  0.7 18.0 %copy-start.14 = (f32[3,700,43]{1,2,0:T(8,128)S(1)}, f32[3,700,43]{1,2,0:T(8,128)}, u32[]{:S(2)}) copy-start(f32[3,700,43]{1,2,0:T(8,128)} %param.35) | copy-start | bytes 1083604
  2.2 16.5 %all-to-all-start = ((s32[32,1,48]{2,1,0:T(1,128)}), s32[32,1,48]{2,1,0:T(1,128)S(1)}, u32[]{:S(2)}, u32[]{:S(2)}) async-start(s32[32,1,48]{2,1,0:T(1,128)} %all_to_all.31), calls=%async_computation | async-start | bytes 32768 | tf_op jit(solution)/shard_map/all_to_all | solution.py:158
  14.2 0.8 copy-start.5
  16.4 7.5 %copy-start.1 = (s32[1024]{0:T(1024)S(1)}, s32[1024]{0:T(1024)}, u32[]{:S(2)}) copy-start(s32[1024]{0:T(1024)} %param.20) | copy-start | bytes 12292
  18.7 11.2 %copy-start.16 = (s32[32,1,48]{2,1,0:T(1,128)}, s32[32,1,48]{2,1,0:T(1,128)S(1)}, u32[]{:S(2)}) copy-start(s32[32,1,48]{2,1,0:T(1,128)S(1)} %all-to-all-done) | copy-start | bytes 18436
  19.6 16.9 %all-to-all-start.3 = ((bf16[4,3,700,43]{2,3,1,0:T(8,128)(2,1)}), bf16[4,3,700,43]{2,3,1,0:T(8,128)(2,1)}, u32[]{:S(2)}, u32[]{:S(2)}) async-start(bf16[4,3,700,43]{2,3,1,0:T(8,128)(2,1)} %broadcast_in_dim.93), calls=%async_computation.3 | async-start | bytes 1769472 | tf_op jit(solution)/shard_map/all_to_all | solution.py:34
  35.7 16.2 %copy-start.24 = (s32[512,10]{0,1:T(8,128)S(1)}, s32[512,10]{0,1:T(8,128)}, u32[]{:S(2)}) copy-start(s32[512,10]{0,1:T(8,128)} %param.22) | copy-start | bytes 61444
  35.7 16.2 %copy-start.18 = (bf16[272,272]{1,0:T(8,128)(2,1)S(1)}, bf16[272,272]{1,0:T(8,128)(2,1)}, u32[]{:S(2)}) copy-start(bf16[272,272]{1,0:T(8,128)(2,1)} %param.29) | copy-start | bytes 443908
  35.7 17.0 %copy-start.19 = (bf16[272,272]{1,0:T(8,128)(2,1)S(1)}, bf16[272,272]{1,0:T(8,128)(2,1)}, u32[]{:S(2)}) copy-start(bf16[272,272]{1,0:T(8,128)(2,1)} %param.30) | copy-start | bytes 443908
  35.7 17.9 %copy-start.22 = (s32[512,12]{0,1:T(8,128)S(1)}, s32[512,12]{0,1:T(8,128)}, u32[]{:S(2)}) copy-start(s32[512,12]{0,1:T(8,128)} %param.24) | copy-start | bytes 73732
  35.7 17.9 %copy-start.26 = (f32[100]{0:T(128)S(1)}, f32[100]{0:T(128)}, u32[]{:S(2)}) copy-start(f32[100]{0:T(128)} %param.27) | copy-start | bytes 1204
  35.7 17.9 %copy-start.27 = (f32[100]{0:T(128)S(1)}, f32[100]{0:T(128)}, u32[]{:S(2)}) copy-start(f32[100]{0:T(128)} %param.26) | copy-start | bytes 1204
  36.6 30.3 %all-to-all-start.1 = ((f32[32,48,173]{2,1,0:T(8,128)}), f32[32,48,173]{2,1,0:T(8,128)S(1)}, u32[]{:S(2)}, u32[]{:S(2)}) async-start(f32[32,48,173]{2,1,0:T(8,128)} %pad_maximum_fusion.1), calls=%async_computation.1 | async-start | bytes 3145728 | tf_op jit(solution)/shard_map/all_to_all | solution.py:15
  66.9 53.6 %all-to-all-start.2 = ((bf16[4,512,64]{1,2,0:T(8,128)(2,1)}), bf16[4,512,64]{1,2,0:T(8,128)(2,1)S(1)}, u32[]{:S(2)}, u32[]{:S(2)}) async-start(bf16[4,512,64]{1,2,0:T(8,128)(2,1)} %bitcast.139), calls=%async_computation.2 | async-start | bytes 524288 | tf_op jit(solution)/shard_map/all_to_all | solution.py:174
  71.1 6.4 %copy-start.6 = (s32[512,2]{1,0:T(8,128)S(1)}, s32[512,2]{1,0:T(8,128)}, u32[]{:S(2)}) copy-start(s32[512,2]{1,0:T(8,128)} %copy-done.5) | copy-start | bytes 12292
  117.1 1.9 copy-start.32
  117.1 3.4 %copy-start.11 = (bf16[516,700]{1,0:T(8,128)(2,1)S(1)}, bf16[516,700]{1,0:T(8,128)(2,1)}, u32[]{:S(2)}) copy-start(bf16[516,700]{1,0:T(8,128)(2,1)} %dot_general.51) | copy-start | bytes 2167204
  117.5 1.4 copy-start.3
  119.0 34.8 %copy-start.12 = (bf16[512,172]{0,1:T(8,128)(2,1)}, bf16[512,172]{0,1:T(8,128)(2,1)S(1)}, u32[]{:S(2)}) copy-start(bf16[512,172]{0,1:T(8,128)(2,1)S(1)} %get-tuple-element.7) | copy-start | bytes 528388
  138.1 2.4 %copy-start.9 = (bf16[32,48,1]{2,1,0:T(8,128)(2,1)S(1)}, bf16[32,48,1]{2,1,0:T(8,128)(2,1)}, u32[]{:S(2)}) copy-start(bf16[32,48,1]{2,1,0:T(8,128)(2,1)} %convert_element_type.107) | copy-start | bytes 9220
  142.1 7.0 %copy-start.33 = (f32[4,43]{1,0:T(4,128)S(1)}, f32[4,43]{1,0:T(4,128)}, u32[]{:S(2)}) copy-start(f32[4,43]{1,0:T(4,128)} %param.37) | copy-start | bytes 2068
  142.1 7.6 %copy-start.4 = (f32[1024,172]{0,1:T(8,128)S(1)}, f32[1024,172]{0,1:T(8,128)}, u32[]{:S(2)}) copy-start(f32[1024,172]{0,1:T(8,128)} %param.19) | copy-start | bytes 2113540
  142.1 7.6 %copy-start.23 = (f32[3,172,43]{1,2,0:T(8,128)S(1)}, f32[3,172,43]{1,2,0:T(8,128)}, u32[]{:S(2)}) copy-start(f32[3,172,43]{1,2,0:T(8,128)} %param.36) | copy-start | bytes 266260
  142.1 9.2 %copy-start.17 = (s32[32,1,48]{2,1,0:T(1,128)S(1)}, s32[32,1,48]{2,1,0:T(1,128)}, u32[]{:S(2)}) copy-start(s32[32,1,48]{2,1,0:T(1,128)} %copy-done.16) | copy-start | bytes 18436
  142.1 33.9 %all-to-all-start.4 = ((bf16[32,48,517]{2,1,0:T(8,128)(2,1)}), bf16[32,48,517]{2,1,0:T(8,128)(2,1)S(1)}, u32[]{:S(2)}, u32[]{:S(2)}) async-start(bf16[32,48,517]{2,1,0:T(8,128)(2,1)} %pad_maximum_fusion), calls=%async_computation.4 | async-start | bytes 3932160 | tf_op jit(solution)/shard_map/all_to_all | solution.py:15
  150.7 3.5 %copy-start.21 = (bf16[272,272]{0,1:T(8,128)(2,1)S(1)}, bf16[272,272]{0,1:T(8,128)(2,1)}, u32[]{:S(2)}) copy-start(bf16[272,272]{0,1:T(8,128)(2,1)} %copy.83) | copy-start | bytes 443908
  152.0 24.5 %copy-start.25 = (s32[1536]{0:T(1024)}, s32[1536]{0:T(1024)S(1)}, u32[]{:S(2)}) copy-start(s32[1536]{0:T(1024)S(1)} %reshape.240) | copy-start | bytes 18436
  152.0 2.2 copy-start.10
  153.7 2.2 copy-start.8
  154.2 38.4 %copy-start.20 = (bf16[272,272]{0,1:T(8,128)(2,1)S(1)}, bf16[272,272]{0,1:T(8,128)(2,1)}, u32[]{:S(2)}) copy-start(bf16[272,272]{0,1:T(8,128)(2,1)} %copy.84) | copy-start | bytes 443908
  176.0 20.9 %copy-start.2 = (bf16[32,48,517]{2,1,0:T(8,128)(2,1)}, bf16[32,48,517]{2,1,0:T(8,128)(2,1)S(1)}, u32[]{:S(2)}) copy-start(bf16[32,48,517]{2,1,0:T(8,128)(2,1)S(1)} %all-to-all-done.4) | copy-start | bytes 4764676
  188.3 24.6 %all-to-all-start.5 = ((bf16[4,2,512]{2,1,0:T(2,128)(2,1)}), bf16[4,2,512]{2,1,0:T(2,128)(2,1)}, u32[]{:S(2)}, u32[]{:S(2)}) async-start(bf16[4,2,512]{2,1,0:T(2,128)(2,1)} %reshape.296), calls=%async_computation.5 | async-start | bytes 16384 | tf_op jit(solution)/shard_map/all_to_all | solution.py:49
  211.7 5.5 %copy-start.13 = (bf16[512,172]{0,1:T(8,128)(2,1)S(1)}, bf16[512,172]{0,1:T(8,128)(2,1)}, u32[]{:S(2)}) copy-start(bf16[512,172]{0,1:T(8,128)(2,1)} %copy-done.12) | copy-start | bytes 528388
  211.7 5.5 %copy-start.34 = (bf16[444,172]{0,1:T(8,128)(2,1)S(1)}, bf16[444,172]{0,1:T(8,128)(2,1)}, u32[]{:S(2)}) copy-start(bf16[444,172]{0,1:T(8,128)(2,1)} %param.31) | copy-start | bytes 458212
  211.7 5.5 %copy-start.35 = (bf16[172,172]{1,0:T(8,128)(2,1)S(1)}, bf16[172,172]{1,0:T(8,128)(2,1)}, u32[]{:S(2)}) copy-start(bf16[172,172]{1,0:T(8,128)(2,1)} %param.33) | copy-start | bytes 177508
  211.7 5.5 %copy-start.36 = (f32[172]{0:T(256)S(1)}, f32[172]{0:T(256)}, u32[]{:S(2)}) copy-start(f32[172]{0:T(256)} %param.34) | copy-start | bytes 2068
  211.8 5.5 %copy-start.37 = (f32[172]{0:T(256)S(1)}, f32[172]{0:T(256)}, u32[]{:S(2)}) copy-start(f32[172]{0:T(256)} %param.32) | copy-start | bytes 2068
  211.8 5.5 %copy-start.38 = (bf16[512,2,136]{0,2,1:T(8,128)(2,1)S(1)}, bf16[512,2,136]{0,2,1:T(8,128)(2,1)}, u32[]{:S(2)}) copy-start(bf16[512,2,136]{0,2,1:T(8,128)(2,1)} %multiply_reduce_fusion) | copy-start | bytes 835588
  212.9 19.3 %all-to-all-start.6 = ((bf16[4,1024,3,43]{1,3,2,0:T(8,128)(2,1)}), bf16[4,1024,3,43]{1,3,2,0:T(8,128)(2,1)S(1)}, u32[]{:S(2)}, u32[]{:S(2)}) async-start(bf16[4,1024,3,43]{1,3,2,0:T(8,128)(2,1)} %copy.91), calls=%async_computation.6 | async-start | bytes 2359296 | tf_op jit(solution)/shard_map/all_to_all | solution.py:49
  217.2 15.3 %copy-start.7 = (f32[3,1024,43]{1,2,0:T(8,128)S(1)}, f32[3,1024,43]{1,2,0:T(8,128)}, u32[]{:S(2)}) copy-start(f32[3,1024,43]{1,2,0:T(8,128)} %convolution_bitcast_fusion) | copy-start | bytes 1585156
  217.2 15.3 %copy-start.28 = (f32[43]{0:T(128)S(1)}, f32[43]{0:T(128)}, u32[]{:S(2)}) copy-start(f32[43]{0:T(128)} %get-tuple-element.11) | copy-start | bytes 520
  217.2 15.3 %copy-start.29 = (f32[43]{0:T(128)S(1)}, f32[43]{0:T(128)}, u32[]{:S(2)}) copy-start(f32[43]{0:T(128)} %get-tuple-element.12) | copy-start | bytes 520
  217.2 15.3 %copy-start.30 = (f32[43]{0:T(128)S(1)}, f32[43]{0:T(128)}, u32[]{:S(2)}) copy-start(f32[43]{0:T(128)} %get-tuple-element.13) | copy-start | bytes 520
  217.2 15.3 %copy-start.31 = (f32[43]{0:T(128)S(1)}, f32[43]{0:T(128)}, u32[]{:S(2)}) copy-start(f32[43]{0:T(128)} %get-tuple-element.14) | copy-start | bytes 520
where the time goes:
time: 236 us; the launch traced here: 233 us
  local copies, waits for them, and re-layouts  81 us (34%)
  other arithmetic  58.8 us (25%)
  starting transfers between devices  40.6 us (17%)
  waiting for transfers between devices  35.5 us (15%)
  matrix products  16.2 us (7%)
    gather x3, local copies, waits for them, and re-layouts, per_device(): picked = jnp.take(fetched, slot_ref, axis=0)  39.1 us
    scatter-add x2, other arithmetic, sum_rows(): sums = jax.ops.segment_sum(source_vals, lookup, num_segments=total)  21.7 us
    all_to_all x2, waiting for transfers between devices, sent_together(): lax.all_to_all(both, axis, split_axis=split_dim, concat_axis=concat_dim,...  20.7 us
    scatter-add x2, other arithmetic, sum_rows(): hit_counts = jax.ops.segment_sum(weights, lookup, num_segments=total)  16 us
    all_to_all x2, starting transfers between devices, sent_together(): lax.all_to_all(both, axis, split_axis=split_dim, concat_axis=concat_dim,...  14.6 us
    all_to_all x2, waiting for transfers between devices, summed_on_arrival(): lax.all_to_all(pieces, axis, split_axis=0, concat_axis=0, tiled=True)  13 us
    all_to_all x1, starting transfers between devices, per_device(): lax.all_to_all(slot_rows.reshape(node_count, per_owner), 'node', split_ax...  9.59 us
    another operation x2, other arithmetic  8.61 us
  transfers between devices with their start and end apart: 7, of which 5 were waited for; matrix products, arithmetic and copies ran while one was open for 50% of the time, Pallas kernels for 0%

commit v1 on v0

v1 whole, which is shorter than its diff:
```python
import functools
import math

import jax
import jax.numpy as jnp
from jax import lax
from jax.experimental import pallas as pl
from jax.experimental.pallas import tpu as pltpu
from jax.sharding import PartitionSpec as P

F32, BF16, I32 = jnp.float32, jnp.bfloat16, jnp.int32
MESH = pl.DeviceIdType.MESH
COS = (
    0.9999999998851011,
    -0.49999999850736465,
    0.041666663483369594,
    -0.0013888863001969808,
    2.4800551963260593e-05,
    -2.7534774132807624e-07,
    2.060335926598073e-09,
    -9.721760760713551e-12,
)
TURN_HI = 6.28125
TURN_LO = 2.0 * math.pi - TURN_HI

MEM, TIME, ATT, EMB, UNITS = 172, 100, 272, 172, 43
CAP, K, EV, ROWS, SLOTS = 48, 10, 512, 1024, 1536
HEAD = ATT // 2
GROUPS, PEERS = 4, 32


def cosine(x):
    turns = jnp.floor(x * (0.5 / math.pi) + 0.5)
    r = (x - turns * TURN_HI) - turns * TURN_LO
    u = r * r
    total = jnp.full_like(u, COS[-1])
    for c in COS[-2::-1]:
        total = total * u + c
    return total


def mm(a, b):
    return jnp.dot(a, b, preferred_element_type=F32)


def mm_nt(a, b):
    return lax.dot_general(a, b, (((1,), (1,)), ((), ())), preferred_element_type=F32)


def iota(shape, dim):
    return lax.broadcasted_iota(I32, shape, dim)


def one_hot(mask):
    return jnp.where(mask, 1.0, 0.0).astype(BF16)


def kernel(
    memory,
    last_update,
    ev_time,
    nbr_gap,
    slot_rows,
    slot_ref,
    edge_feat,
    frequency,
    phase_shift,
    w_query,
    w_key,
    w_value,
    w_merge,
    b_merge,
    w_out,
    b_out,
    w_input,
    w_hidden,
    gru_bias,
    embedding,
    new_memory,
    req_send,
    req_recv,
    row_send,
    fetched,
    edge_recv,
    w_mine,
    wx_mine,
    w_all,
    wx_all,
    main_send,
    main_recv,
    ext_send,
    ext_recv,
    vec,
    memb,
    tail,
    small,
    times,
    wkv,
    wq,
    wm,
    zed,
    own,
    req_lanes,
    end_cols,
    hits,
    src,
    msg,
    ext_tmp,
    query,
    hot,
    near,
    kv,
    att,
    acc,
    send_sem,
    recv_req,
    recv_rows,
    recv_x,
    recv_main,
    recv_ext,
):
    n = lax.axis_index("node")
    f = lax.axis_index("feat")
    y, z, c = n // 8, (n // 2) % 4, n % 2

    def peer(dy, j, dx):
        to = ((y + dy) % 4) * 8 + ((z + j // 2) % 4) * 2 + (c + j % 2) % 2
        return to, (f + dx) % 4

    def send(src_ref, dst_ref, s_sem, r_sem, to):
        pltpu.make_async_remote_copy(
            src_ref=src_ref,
            dst_ref=dst_ref,
            send_sem=s_sem,
            recv_sem=r_sem,
            device_id=to,
            device_id_type=MESH,
        ).start()

    def wait_bytes(ref, sem):
        pltpu.make_async_copy(ref, ref, sem).wait()

    barrier = pltpu.get_barrier_semaphore()

    def greet(i, carry):
        to = peer(i // 32, i % 8, (i // 8) % 4)
        pl.semaphore_signal(barrier, inc=1, device_id=to, device_id_type=MESH)
        return carry

    lax.fori_loop(1, 128, greet, 0)

    req_send[...] = jnp.full(req_send.shape, -1, I32)
    for o in range(32):
        req_send[o, :, 0:CAP] = slot_rows[:, o * CAP : (o + 1) * CAP]
    req_recv[0] = req_send[n]
    edge_recv[f] = edge_feat[pl.ds(pl.multiple_of(f * EV, EV), EV), :]

    pl.semaphore_wait(barrier, 127)

    def ask(i, carry):
        dy, dx, j = i // 32, (i // 8) % 4, i % 8
        to = peer(dy, j, dx)
        send(req_send.at[to[0]], req_recv.at[i], send_sem.at[0], recv_req.at[1], to)
        return carry

    for dy in range(4):
        for j in range(8):
            if dy == 0 and j == 0:
                continue
            to = peer(dy, j, 0)
            send(
                req_send.at[to[0]],
                req_recv.at[dy * 32 + j],
                send_sem.at[0],
                recv_req.at[2 + dy],
                to,
            )
    for dy in range(4):
        lax.fori_loop(dy * 32 + 8, dy * 32 + 32, ask, 0)

    for dx in range(1, 4):
        to = peer(0, 0, dx)
        send(
            edge_feat.at[pl.ds(pl.multiple_of(to[1] * EV, EV), EV), :],
            edge_recv.at[f],
            send_sem.at[1],
            recv_x.at[0],
            to,
        )

    small[...] = jnp.zeros(small.shape, F32)
    small[0:8, :] = last_update[...].astype(F32)
    stamp_cols = small[...].T
    tail[:, 0:44] = memory[:, 128:MEM]
    lane = iota((128, 128), 1)
    memb[:, 0:128] = memory[:, 0:128].astype(BF16)
    for b in range(8):
        stamp = stamp_cols[:, b : b + 1]
        high = jnp.floor(stamp * (1.0 / 128.0))
        low = stamp - high * 128.0
        part = tail[b * 128 : (b + 1) * 128, :]
        part = jnp.where(
            lane < 44, part, jnp.where(lane == 44, high, jnp.where(lane == 45, low, 0.0))
        )
        memb[b * 128 : (b + 1) * 128, 128:256] = part.astype(BF16)

    r640 = iota((640, 700), 0)
    c640 = iota((640, 700), 1)
    picked = (
        ((r640 < MEM) & (c640 == r640 + MEM))
        | ((r640 >= 256) & (r640 < 256 + TIME) & (c640 == r640 - 256 + 2 * MEM))
        | ((r640 >= 384) & (c640 == r640 - 384 + 2 * MEM + TIME))
    )
    place = one_hot(picked)
    rows43 = iota((UNITS, 128), 0)
    cols43 = iota((UNITS, 128), 1)
    wide = mm(w_input[0].astype(BF16), one_hot(cols43 == rows43))
    wide += mm(w_input[1].astype(BF16), one_hot(cols43 == rows43 + UNITS))
    wide += mm(w_input[2].astype(BF16), one_hot(cols43 == rows43 + 2 * UNITS))
    w_mine[...] = mm(place, wide.astype(BF16)).astype(BF16)
    last = mm_nt(one_hot(iota((8, UNITS), 1) == UNITS - 1), w_input[2].astype(BF16))
    wx_mine[...] = mm_nt(last.astype(BF16), place)[0:1, :]
    w_all[0] = w_mine[...]
    wx_all[0] = wx_mine[...]
    for dx in range(1, 4):
        to = peer(0, 0, 4 - dx)
        send(w_mine, w_all.at[dx], send_sem.at[2], recv_x.at[1], to)
        send(wx_mine, wx_all.at[dx], send_sem.at[3], recv_x.at[2], to)

    for dy in range(4):
        first = 1 if dy == 0 else 0
        wait_bytes(req_recv.at[dy * 32 + first : dy * 32 + 8], recv_req.at[2 + dy])
    for dy in range(4):
        small[8 * dy : 8 * dy + 8, :] = req_recv[dy * 32 : dy * 32 + 8].reshape(8, 128).astype(F32)
    asked = small[...].T.astype(I32)
    row_lane = iota((CAP, ROWS), 1)
    for dy in range(4):
        mask = jnp.concatenate(
            [
                one_hot(asked[0:CAP, 8 * dy + j : 8 * dy + j + 1] == row_lane)
                for j in range(8)
            ],
            axis=0,
        )
        rows = mm(mask, memb[...]).astype(BF16)
        for j in range(8):
            piece = rows[j * CAP : (j + 1) * CAP, :]
            if dy == 0 and j == 0:
                fetched[n] = piece
            else:
                row_send[dy * 8 + j] = piece
                to_n = ((y - dy + 4) % 4) * 8 + ((z - j // 2 + 4) % 4) * 2 + (c + j % 2) % 2
                send(
                    row_send.at[dy * 8 + j],
                    fetched.at[n],
                    send_sem.at[4],
                    recv_rows,
                    (to_n, f),
                )

    vec[...] = jnp.zeros(vec.shape, F32)
    vec[0:1, 0:TIME] = frequency[...]
    vec[1:2, 0:TIME] = phase_shift[...]
    vec[2:3, 0:EMB] = b_merge[...]
    vec[3:4, 0:EMB] = b_out[...]
    vec[4:8, 0:UNITS] = gru_bias[...]
    freq = vec[0:1, 0:128]
    phase = vec[1:2, 0:128]

    for k in range(K):
        times[k] = cosine(nbr_gap[:, k : k + 1].astype(F32) * freq + phase).astype(BF16)

    r272 = iota((384, ATT), 0)
    c272 = iota((384, ATT), 1)
    place = one_hot(
        ((c272 < MEM) & (r272 == c272)) | ((c272 >= MEM) & (r272 == c272 + (256 - MEM)))
    )
    wkv[...] = jnp.zeros(wkv.shape, BF16)
    wkv[:, 0:ATT] = mm(place, w_key[...]).astype(BF16)
    wkv[:, 384 : 384 + ATT] = mm(place, w_value[...]).astype(BF16)
    wq[...] = jnp.zeros(wq.shape, BF16)
    wq[:, 0:ATT] = mm(place, w_query[...]).astype(BF16)
    r444 = iota((640, ATT + MEM), 0)
    c444 = iota((640, ATT + MEM), 1)
    place = one_hot(
        ((c444 < ATT) & (r444 == c444)) | ((c444 >= ATT) & (r444 == c444 + (384 - ATT)))
    )
    wm[...] = mm(place, w_merge[...]).astype(BF16)

    tail[...] = jnp.zeros(tail.shape, F32)
    tail[0:EV, 0 : K + 2] = slot_ref[...].astype(F32)
    cols = tail[0:EV, :].T.astype(I32)
    end_cols[:, 0:EV] = cols[0:1, :]
    end_cols[:, EV : 2 * EV] = cols[1:2, :]

    wait_bytes(fetched.at[0:31], recv_rows)
    table = fetched.reshape(SLOTS, 256)

    slot_lane = iota((256, SLOTS), 1)
    count = jnp.zeros((1, SLOTS), F32)
    for b in range(2):
        picks = slot_ref[b * 256 : (b + 1) * 256, :]
        for e in range(2):
            mask = jnp.where(picks[:, e : e + 1] == slot_lane, 1.0, 0.0)
            count += jnp.sum(mask, axis=0, keepdims=True)
            src[e, b * 256 : (b + 1) * 256, :] = mm(mask.astype(BF16), table[...])
    hits[...] = count

    small[...] = jnp.zeros(small.shape, F32)
    small[0:4, :] = ev_time[...].astype(F32)
    ev_cols = small[...].T
    lane = iota((EV, 128), 1)
    wait_bytes(edge_recv.at[0:3], recv_x.at[0])
    for half in range(2):
        pair = jnp.concatenate(
            [edge_recv[2 * half].astype(F32), edge_recv[2 * half + 1].astype(F32)], axis=1
        ).astype(BF16)
        for e in range(2):
            msg[e * EV : (e + 1) * EV, 384 + half * 128 : 512 + half * 128] = pair
    for e in range(2):
        msg[e * EV : (e + 1) * EV, 0:256] = src[1 - e].astype(BF16)
        for b in range(4):
            stamp = (
                src[e, b * 128 : (b + 1) * 128, MEM : MEM + 1] * 128.0
                + src[e, b * 128 : (b + 1) * 128, MEM + 1 : MEM + 2]
            )
            gap = ev_cols[:, b : b + 1] - stamp
            msg[e * EV + b * 128 : e * EV + (b + 1) * 128, 256:384] = cosine(
                gap * freq + phase
            ).astype(BF16)

    wait_bytes(w_all.at[0:3], recv_x.at[1])
    wait_bytes(wx_all.at[0:3], recv_x.at[2])
    ext_send[...] = jnp.zeros(ext_send.shape, F32)

    def give(step, carry):
        dy = (step + 1) % 4
        base = ((y + dy) % 4) * 384
        mask = one_hot(iota((384, 2 * EV), 0) + base == end_cols[...])
        sums = mm(mask, msg[...]).astype(BF16)
        for pair in range(2):
            w_pair = jnp.concatenate([w_all[2 * pair], w_all[2 * pair + 1]], axis=1)
            out = mm(sums, w_pair).astype(BF16)
            for i in range(2):
                main_send[dy, 2 * pair + i] = out[:, i * 128 : (i + 1) * 128].reshape(8, CAP, 128)
        rows4 = jnp.concatenate(
            [wx_all[dx] for dx in range(4)] + [jnp.zeros((4, 640), F32)], axis=0
        )
        ext_tmp[0:8, :] = mm_nt(rows4.astype(BF16), sums)
        ext_tmp[8:9, :] = hits[:, pl.ds(pl.multiple_of(base, 128), 384)]
        for j in range(8):
            count_row = ext_tmp[8:9, j * CAP : (j + 1) * CAP]
            for dx in range(4):
                ext_send[dy, dx, j, :, 0:CAP] = ext_tmp[dx : dx + 1, j * CAP : (j + 1) * CAP]
                ext_send[dy, dx, j, :, 64 : 64 + CAP] = count_row

        def post(i, inner):
            dx, j = i % 4, i // 4
            to = peer(dy, j, dx)
            at = to[0] % 8
            send(
                main_send.at[dy, dx, at],
                main_recv.at[dy, dx * 8 + j],
                send_sem.at[5],
                recv_main.at[dy],
                to,
            )
            send(
                ext_send.at[dy, dx, at],
                ext_recv.at[dy, dx * 8 + j],
                send_sem.at[6],
                recv_ext.at[dy],
                to,
            )
            return inner

        lax.fori_loop(jnp.where(dy == 0, 1, 0), 32, post, 0)
        return carry

    lax.fori_loop(0, 4, give, 0)
    main_recv[0, 0] = main_send[0, 0, n % 8]
    ext_recv[0, 0] = ext_send[0, 0, n % 8]

    still = jnp.broadcast_to(cosine(phase), (EV, 128)).astype(BF16)
    query[...] = (
        mm(src[0].astype(BF16), wq[0:256, :]) + mm(still, wq[256:384, :])
    ) * (1.0 / math.sqrt(HEAD))
    lane_q = iota((16, 384), 1)
    first_head = lane_q < HEAD
    slot_lane = iota((128, SLOTS), 1)

    def attend(b, carry):
        at = pl.multiple_of(b * 128, 128)
        picks = slot_ref[pl.ds(at, 128), :]
        for k in range(K):
            hot[k * 128 : (k + 1) * 128, :] = one_hot(picks[:, 2 + k : 3 + k] == slot_lane)
        near[...] = mm(hot[...], table[...]).astype(BF16)
        code = times[:, pl.ds(at, 128), :].reshape(K * 128, 128)
        kv[...] = (mm(near[...], wkv[0:256, :]) + mm(code, wkv[256:384, :])).reshape(K, 128, 768)

        def group(g, inner):
            r = pl.multiple_of(g * 16, 16)
            q = query[pl.ds(at + r, 16), :]
            s0, s1 = [], []
            for k in range(K):
                t = q * kv[k, pl.ds(r, 16), 0:384]
                s0.append(jnp.sum(jnp.where(first_head, t, 0.0), axis=1, keepdims=True))
                s1.append(jnp.sum(jnp.where(first_head, 0.0, t), axis=1, keepdims=True))
            m0 = functools.reduce(jnp.maximum, s0)
            m1 = functools.reduce(jnp.maximum, s1)
            p0 = [jnp.exp(s - m0) for s in s0]
            p1 = [jnp.exp(s - m1) for s in s1]
            total = jnp.zeros((16, 384), F32)
            for k in range(K):
                w = jnp.where(first_head, p0[k], p1[k])
                total += w * kv[k, pl.ds(r, 16), 384:768]
            norm = jnp.where(first_head, sum(p0), sum(p1))
            att[pl.ds(at + r, 16), :] = (total / norm).astype(BF16)
            return inner

        lax.fori_loop(0, 8, group, 0)
        return carry

    lax.fori_loop(0, 4, attend, 0)
    hidden = mm(att[...], wm[0:384, :]) + mm(src[0].astype(BF16), wm[384:640, :])
    hidden = jnp.maximum(hidden + vec[2:3, 0:EMB], 0.0).astype(BF16)
    embedding[...] = (mm(hidden, w_out[...]) + vec[3:4, 0:EMB]).astype(BF16)

    rows172 = iota((UNITS, 128), 0)
    cols172 = iota((UNITS, 128), 1)
    widen = one_hot(rows172 == cols172)
    pad = one_hot(iota((256, MEM), 0) == iota((256, MEM), 1))
    gates = (
        w_input[0, 0:MEM, :] + w_hidden[0],
        w_input[1, 0:MEM, :] + w_hidden[1],
        w_input[2, 0:MEM, :],
        w_hidden[2],
    )
    for g, w in enumerate(gates):
        w_wide = mm(w.astype(BF16), widen).astype(BF16)
        zed[g] = mm(memb[...], mm(pad, w_wide).astype(BF16))
    own[...] = jnp.dot(
        memory[...],
        jnp.where(
            (iota((MEM, 128), 0) == iota((MEM, 128), 1) + f * UNITS) & (iota((MEM, 128), 1) < UNITS),
            1.0,
            0.0,
        ),
        preferred_element_type=F32,
        precision=lax.Precision.HIGHEST,
    )

    wait_bytes(req_recv.at[0:96], recv_req.at[1])
    for i in range(128):
        dy, j = i // 32, i % 32
        req_lanes[dy, :, j * CAP : (j + 1) * CAP] = req_recv[i, :, 0:CAP]

    acc[...] = jnp.zeros(acc.shape, F32)
    lane48 = iota((CAP, 128), 1)
    for dy in (1, 2, 3, 0):
        first = 1 if dy == 0 else 0
        wait_bytes(main_recv.at[dy, first:32], recv_main.at[dy])
        wait_bytes(ext_recv.at[dy, first:32], recv_ext.at[dy])
        small[...] = jnp.zeros(small.shape, F32)
        small[0:32, :] = ext_recv[dy].reshape(32, 128)
        ext_t = small[...].T
        count = ext_t[64 : 64 + CAP, :]
        high = jnp.floor(count * (1.0 / 128.0))
        low = count - high * 128.0
        both = jnp.where(
            lane48 < 32,
            ext_t[0:CAP, :],
            jnp.where(
                lane48 < 64,
                pltpu.roll(low, 32, axis=1),
                jnp.where(lane48 < 96, pltpu.roll(high, 64, axis=1), 0.0),
            ),
        )
        side = jnp.concatenate(
            [jnp.where(lane48 % 32 == i, both, 0.0).astype(BF16) for i in range(32)], axis=0
        )
        right = jnp.concatenate([main_recv[dy].reshape(SLOTS, 128), side], axis=1)
        for b in range(4):
            mask = one_hot(iota((256, SLOTS), 0) + b * 256 == req_lanes[dy])
            acc[b * 256 : (b + 1) * 256, :] += mm(mask, right)

    lane = iota((256, 128), 1)
    for b in range(4):
        at = slice(b * 256, (b + 1) * 256)
        main = acc[at, 0:128]
        extra = acc[at, 128:256]
        last_unit = jnp.sum(jnp.where(lane < 32, extra, 0.0), axis=1, keepdims=True)
        heard = jnp.sum(
            jnp.where(
                (lane >= 32) & (lane < 64),
                extra,
                jnp.where((lane >= 64) & (lane < 96), extra * 128.0, 0.0),
            ),
            axis=1,
            keepdims=True,
        )
        share = 1.0 / jnp.maximum(heard, 1.0)
        i1 = pltpu.roll(main, 128 - UNITS, axis=1)
        i2 = jnp.where(lane == UNITS - 1, last_unit, pltpu.roll(main, 128 - 2 * UNITS, axis=1))
        b0, b1, b2, b3 = (vec[4 + g : 5 + g, 0:128] for g in range(4))
        reset = jax.nn.sigmoid(main * share + zed[0, at, :] + b0)
        update = jax.nn.sigmoid(i1 * share + zed[1, at, :] + b1)
        cand = jnp.tanh(i2 * share + zed[2, at, :] + b2 + reset * (zed[3, at, :] + b3))
        mine = own[at, :]
        fresh = (1.0 - update) * cand + update * mine
        new_memory[at, :] = jnp.where(heard > 0.0, fresh, mine)[:, 0:UNITS]

    wait_bytes(req_recv.at[0:127], send_sem.at[0])
    wait_bytes(edge_recv.at[0:3], send_sem.at[1])
    wait_bytes(w_all.at[0:3], send_sem.at[2])
    wait_bytes(wx_all.at[0:3], send_sem.at[3])
    wait_bytes(row_send.at[0:31], send_sem.at[4])
    wait_bytes(main_recv.at[0:3], send_sem.at[5])
    wait_bytes(main_recv.at[3, 0:31], send_sem.at[5])
    wait_bytes(ext_recv.at[0:3], send_sem.at[6])
    wait_bytes(ext_recv.at[3, 0:31], send_sem.at[6])


def step(
    memory,
    last_update,
    ev_time,
    nbr_gap,
    slot_rows,
    slot_ref,
    edge_feat,
    frequency,
    phase_shift,
    w_query,
    w_key,
    w_value,
    w_merge,
    b_merge,
    w_out,
    b_out,
    w_input,
    w_hidden,
    gru_bias,
):
    args = (
        memory,
        last_update.reshape(8, 128),
        ev_time.reshape(4, 128),
        nbr_gap,
        slot_rows,
        slot_ref,
        edge_feat,
        frequency.reshape(1, TIME),
        phase_shift.reshape(1, TIME),
        w_query,
        w_key,
        w_value,
        w_merge,
        b_merge.reshape(1, EMB),
        w_out,
        b_out.reshape(1, EMB),
        w_input,
        w_hidden,
        gru_bias,
    )
    vmem = pl.BlockSpec(memory_space=pltpu.VMEM)
    V, D = pltpu.VMEM, pltpu.SemaphoreType.DMA
    return pl.pallas_call(
        kernel,
        out_shape=(
            jax.ShapeDtypeStruct((EV, EMB), BF16),
            jax.ShapeDtypeStruct((ROWS, UNITS), F32),
        ),
        in_specs=[vmem] * len(args),
        out_specs=(vmem, vmem),
        scratch_shapes=[
            V((32, 1, 128), I32),
            V((128, 1, 128), I32),
            V((32, CAP, 256), BF16),
            V((32, CAP, 256), BF16),
            V((4, EV, 64), BF16),
            V((640, 128), BF16),
            V((1, 640), F32),
            V((4, 640, 128), BF16),
            V((4, 1, 640), F32),
            V((4, 4, 8, CAP, 128), BF16),
            V((4, 32, CAP, 128), BF16),
            V((4, 4, 8, 1, 128), F32),
            V((4, 32, 1, 128), F32),
            V((8, 256), F32),
            V((ROWS, 256), BF16),
            V((ROWS, 128), F32),
            V((128, 128), F32),
            V((K, EV, 128), BF16),
            V((384, 768), BF16),
            V((384, 384), BF16),
            V((640, EMB), BF16),
            V((4, ROWS, 128), F32),
            V((ROWS, 128), F32),
            V((4, 1, SLOTS), I32),
            V((1, 2 * EV), I32),
            V((1, SLOTS), F32),
            V((2, EV, 256), F32),
            V((2 * EV, 640), BF16),
            V((16, 384), F32),
            V((EV, 384), F32),
            V((K * 128, SLOTS), BF16),
            V((K * 128, 256), BF16),
            V((K, 128, 768), F32),
            V((EV, 384), BF16),
            V((ROWS, 256), F32),
            D((7,)),
            D((6,)),
            D,
            D((3,)),
            D((4,)),
            D((4,)),
        ],
        compiler_params=pltpu.CompilerParams(
            collective_id=0, has_side_effects=True, vmem_limit_bytes=60 * 1024 * 1024
        ),
    )(*args)


def solution(mesh):
    return jax.shard_map(
        step,
        mesh=mesh,
        in_specs=(
            P("node", None),
            P("node"),
            P(("node", "feat")),
            P(("node", "feat"), None),
            P(("node", "feat"), None),
            P(("node", "feat"), None),
            P("node", "feat"),
            P(),
            P(),
            P(),
            P(),
            P(),
            P(),
            P(),
            P(),
            P(),
            P(None, None, "feat"),
            P(None, None, "feat"),
            P(None, "feat"),
        ),
        out_specs=(P(("node", "feat"), None), P("node", "feat")),
        check_vma=False,
    )
```

time: 236 us -> 94.8 us (0.40)
  Pallas kernels: 0 us -> 80.5 us
  local copies, waits for them, and re-layouts: 81 us -> 13.3 us
  other arithmetic: 58.8 us -> 0 us
  starting transfers between devices: 40.6 us -> 0 us
  waiting for transfers between devices: 35.5 us -> 0 us
  matrix products: 16.2 us -> 0 us
    pallas_call x0 -> x1, Pallas kernels: none -> 80.5 us  [step(): pl.pallas_call(kernel, out_shape=(jax.ShapeDtypeStruct((EV, EMB), BF16),...]
    gather x8 -> x0, local copies, waits for them, and re-layouts: 55.1 us -> none  [the longest x3 39.1 us: per_device(): picked = jnp.take(fetched, slot_ref, axis=0)]
    all_to_all x7 -> x0, starting transfers between devices: 40.6 us -> none  [the longest x2 14.6 us: sent_together(): lax.all_to_all(both, axis, split_axis=split_dim, concat_axis=concat_dim,...]
    scatter-add x4 -> x0, other arithmetic: 37.8 us -> none  [the longest x2 21.7 us: sum_rows(): sums = jax.ops.segment_sum(source_vals, lookup, num_segments=total)]
    all_to_all x7 -> x0, waiting for transfers between devices: 35.5 us -> none  [the longest x2 20.7 us: sent_together(): lax.all_to_all(both, axis, split_axis=split_dim, concat_axis=concat_dim,...]
    dot_general x6 -> x0, matrix products: 16.2 us -> none  [the longest x1 7.64 us: per_device(): jnp.einsum('en,gnm->egm', message_rows, full_input)]
    another operation x2 -> x0, other arithmetic: 8.61 us -> none
    slice x6 -> x0, local copies, waits for them, and re-layouts: 4.11 us -> none  [the longest x1 1.7 us: per_device(): picked[:, 2:]]
  transfers between devices with their start and end apart: 7 -> 0, of which waited for: 5 -> 0; matrix products, arithmetic and copies ran while one was open for 50% -> 0% of each run, Pallas kernels for 0% -> 0%
where the time goes in v1:
time: 94.8 us; the launch traced here: 94.5 us
  Pallas kernels  80.5 us (85%)
  local copies, waits for them, and re-layouts  13.3 us (14%)
    pallas_call x1, Pallas kernels, step(): pl.pallas_call(kernel, out_shape=(jax.ShapeDtypeStruct((EV, EMB), BF16),...  80.5 us
    unnamed x15, local copies, waits for them, and re-layouts  9.65 us
    pallas_call x2, local copies, waits for them, and re-layouts, step(): pl.pallas_call(kernel, out_shape=(jax.ShapeDtypeStruct((EV, EMB), BF16),...  3.66 us

profile of v1, /device:TPU:1, one launch (start us, length us, event | category | flops | bytes accessed | tf_op | source)
XLA Modules:
  0.0 94.5 jit_solution(16209155737157405557)
XLA Ops:
  0.6 0.0 copy-start.3
  0.6 0.0 copy-start.2
  0.7 0.0 copy-start
  0.7 1.8 %copy.25.w_merge = bf16[444,172]{1,0:T(8,128)(2,1)} copy(bf16[444,172]{0,1:T(8,128)(2,1)} %param.31) | data formatting | bytes 305472 | tf_op args[12]
  2.5 1.6 %copy.22.nbr_gap = s32[512,10]{1,0:T(8,128)} copy(s32[512,10]{0,1:T(8,128)} %param.22) | data formatting | bytes 40960 | tf_op args[3]
  4.1 1.6 %copy.23.slot_ref = s32[512,12]{1,0:T(8,128)} copy(s32[512,12]{0,1:T(8,128)} %param.24) | data formatting | bytes 49152 | tf_op args[5]
  5.7 0.0 copy-done.3
  5.7 0.9 copy.27.w_hidden
  6.5 0.0 copy-done.2
  6.5 1.0 %copy.24.edge_feat = bf16[2048,64]{1,0:T(8,128)(2,1)} copy(bf16[2048,64]{0,1:T(8,128)(2,1)S(1)} %copy-done.2) | data formatting | bytes 524288 | tf_op args[6]
  7.6 0.0 copy-done
  7.6 0.0 copy-start.1
  7.6 1.4 %copy.21.memory = f32[1024,172]{1,0:T(8,128)} copy(f32[1024,172]{0,1:T(8,128)S(1)} %copy-done) | data formatting | bytes 1409024 | tf_op args[0]
  8.9 0.0 copy-done.1
  8.9 1.4 %copy.26.w_input = f32[3,700,43]{2,1,0:T(8,128)} copy(f32[3,700,43]{1,2,0:T(8,128)S(1)} %copy-done.1) | data formatting | bytes 722400 | tf_op args[16]
  10.3 80.5 %shard_map.194 = (bf16[512,172]{1,0:T(8,128)(2,1)}, f32[1024,43]{1,0:T(8,128)}) custom-call(f32[1024,172]{1,0:T(8,128)} %copy.21.memory, s32[8,128]{1,0:T(8,128)} %bitcast.6, s32[4,128]{1,0:T(4,128)} %bitcast.7, s32[512,10]{1,0:T(8,128)} %copy.22.nbr_gap, s32[1,1536]{1,0:T(1,128)} %slot_rows.1, s32[512,12]{1,0:T(8,128)} %copy.23.slot_ref, ...), custom_call_target="tpu_custom_call" | custom-call | tf_op jit(solution)/shard_map/pallas_call | solution.py:568
  90.8 1.7 %copy.28 = bf16[512,172]{0,1:T(8,128)(2,1)} copy(bf16[512,172]{1,0:T(8,128)(2,1)} %get-tuple-element.2) | data formatting | bytes 352256 | tf_op jit(solution)/shard_map/pallas_call | solution.py:568
  92.6 1.9 %copy.29 = f32[1024,43]{0,1:T(8,128)} copy(f32[1024,43]{1,0:T(8,128)} %get-tuple-element.3) | data formatting | bytes 352256 | tf_op jit(solution)/shard_map/pallas_call | solution.py:568
Async XLA Ops:
  0.6 5.0 %copy-start.3 = (f32[3,172,43]{1,2,0:T(8,128)S(1)}, f32[3,172,43]{1,2,0:T(8,128)}, u32[]{:S(2)}) copy-start(f32[3,172,43]{1,2,0:T(8,128)} %param.36) | copy-start | bytes 266260
  0.6 5.9 %copy-start.2 = (bf16[2048,64]{0,1:T(8,128)(2,1)S(1)}, bf16[2048,64]{0,1:T(8,128)(2,1)}, u32[]{:S(2)}) copy-start(bf16[2048,64]{0,1:T(8,128)(2,1)} %param.25) | copy-start | bytes 786436
  0.7 6.9 %copy-start = (f32[1024,172]{0,1:T(8,128)S(1)}, f32[1024,172]{0,1:T(8,128)}, u32[]{:S(2)}) copy-start(f32[1024,172]{0,1:T(8,128)} %param.19) | copy-start | bytes 2113540
  7.6 1.4 %copy-start.1 = (f32[3,700,43]{1,2,0:T(8,128)S(1)}, f32[3,700,43]{1,2,0:T(8,128)}, u32[]{:S(2)}) copy-start(f32[3,700,43]{1,2,0:T(8,128)} %param.35) | copy-start | bytes 1083604

commit v2 on v1

v2 whole, which is shorter than its diff:
```python
import functools
import math

import jax
import jax.numpy as jnp
from jax import lax
from jax.experimental import pallas as pl
from jax.experimental.pallas import tpu as pltpu
from jax.sharding import PartitionSpec as P

F32, BF16, I32 = jnp.float32, jnp.bfloat16, jnp.int32
MESH = pl.DeviceIdType.MESH
COS = (
    0.9999999998851011,
    -0.49999999850736465,
    0.041666663483369594,
    -0.0013888863001969808,
    2.4800551963260593e-05,
    -2.7534774132807624e-07,
    2.060335926598073e-09,
    -9.721760760713551e-12,
)
TURN_HI = 6.28125
TURN_LO = 2.0 * math.pi - TURN_HI

MEM, TIME, ATT, EMB, UNITS = 172, 100, 272, 172, 43
CAP, K, EV, ROWS, SLOTS = 48, 10, 512, 1024, 1536
HEAD = ATT // 2
GROUPS, PEERS = 4, 32


def cosine(x):
    turns = jnp.floor(x * (0.5 / math.pi) + 0.5)
    r = (x - turns * TURN_HI) - turns * TURN_LO
    u = r * r
    total = jnp.full_like(u, COS[-1])
    for c in COS[-2::-1]:
        total = total * u + c
    return total


def mm(a, b):
    return jnp.dot(a, b, preferred_element_type=F32)


def mm_nt(a, b):
    return lax.dot_general(a, b, (((1,), (1,)), ((), ())), preferred_element_type=F32)


def iota(shape, dim):
    return lax.broadcasted_iota(I32, shape, dim)


def one_hot(mask):
    return jnp.where(mask, 1.0, 0.0).astype(BF16)


def kernel(
    memory,
    last_update,
    ev_time,
    nbr_gap,
    slot_rows,
    slot_ref,
    edge_feat,
    frequency,
    phase_shift,
    w_query,
    w_key,
    w_value,
    w_merge,
    b_merge,
    w_out,
    b_out,
    w_input,
    w_hidden,
    gru_bias,
    embedding,
    new_memory,
    req_send,
    req_recv,
    row_send,
    fetched,
    edge_recv,
    w_mine,
    wx_mine,
    w_all,
    wx_all,
    main_send,
    main_recv,
    ext_send,
    ext_recv,
    vec,
    mem_t,
    memb,
    wide_t,
    cols,
    small,
    times,
    wkv,
    wq,
    wm,
    w_ext,
    zed,
    own,
    end_cols,
    hits,
    ends,
    src,
    msg,
    ext_tmp,
    query,
    hot,
    near,
    kv,
    att,
    claims,
    side,
    acc,
    send_sem,
    recv_req,
    recv_rows,
    recv_x,
    recv_main,
    recv_ext,
):
    n = lax.axis_index("node")
    f = lax.axis_index("feat")
    y, z, c = n // 8, (n // 2) % 4, n % 2
    at_y = [((y + d) % 4) * 8 for d in range(4)]
    at_z = [((z + d) % 4) * 2 for d in range(4)]
    at_c = [(c + d) % 2 for d in range(2)]
    at_f = [(f + d) % 4 for d in range(4)]
    in_y = [at_z[j // 2] + at_c[j % 2] for j in range(8)]

    def peer(dy, j, dx):
        return at_y[dy] + in_y[j], at_f[dx]

    def send(src_ref, dst_ref, s_sem, r_sem, to):
        pltpu.make_async_remote_copy(
            src_ref=src_ref,
            dst_ref=dst_ref,
            send_sem=s_sem,
            recv_sem=r_sem,
            device_id=to,
            device_id_type=MESH,
        ).start()

    def wait_bytes(ref, sem):
        pltpu.make_async_copy(ref, ref, sem).wait()

    everyone = [(dy, dx, j) for dy in range(4) for dx in range(4) for j in range(8)][1:]

    for dx in range(4):
        w_all[dx, 176:256, :] = jnp.zeros((80, 128), BF16)
        w_all[dx, 368:384, :] = jnp.zeros((16, 128), BF16)

    barrier = pltpu.get_barrier_semaphore()
    for dy, dx, j in everyone:
        pl.semaphore_signal(
            barrier, inc=1, device_id=peer(dy, j, dx), device_id_type=MESH
        )

    req_send[...] = jnp.full(req_send.shape, -1, I32)
    for o in range(32):
        req_send[o, :, 0:CAP] = slot_rows[:, o * CAP : (o + 1) * CAP]
    req_recv[0] = req_send[n]
    edge_recv[f] = edge_feat[:, pl.ds(pl.multiple_of(f * EV, EV), EV)]

    mem_t[0:MEM, :] = memory[...]
    stamp = last_update[...].astype(F32)
    high = jnp.floor(stamp * (1.0 / 128.0))
    mem_t[MEM : MEM + 1, :] = high
    mem_t[MEM + 1 : MEM + 2, :] = stamp - high * 128.0
    mem_t[MEM + 2 : 256, :] = jnp.zeros((256 - MEM - 2, ROWS), F32)
    for b in range(4):
        memb[b * 256 : (b + 1) * 256, :] = mem_t[:, b * 256 : (b + 1) * 256].T.astype(BF16)

    pl.semaphore_wait(barrier, 127)

    for dy, dx, j in everyone:
        if dx == 0:
            to = peer(dy, j, 0)
            send(
                req_send.at[to[0]],
                req_recv.at[dy * 32 + j],
                send_sem.at[0],
                recv_req.at[2 + dy],
                to,
            )
    for dx in range(1, 4):
        to = peer(0, 0, dx)
        send(
            edge_feat.at[:, pl.ds(pl.multiple_of(to[1] * EV, EV), EV)],
            edge_recv.at[f],
            send_sem.at[1],
            recv_x.at[0],
            to,
        )

    r640 = iota((640, 700), 0)
    c640 = iota((640, 700), 1)
    place = one_hot(
        ((r640 < MEM) & (c640 == r640 + MEM))
        | ((r640 >= 256) & (r640 < 256 + TIME) & (c640 == r640 - 256 + 2 * MEM))
        | ((r640 >= 384) & (c640 == r640 - 384 + 2 * MEM + TIME))
    )
    rows43 = iota((128, UNITS), 0)
    cols43 = iota((128, UNITS), 1)
    wide = mm(one_hot(rows43 == cols43), w_input[0].astype(BF16))
    wide += mm(one_hot(rows43 == cols43 + UNITS), w_input[1].astype(BF16))
    wide += mm(one_hot(rows43 == cols43 + 2 * UNITS), w_input[2].astype(BF16))
    w_mine[...] = mm_nt(place, wide.astype(BF16)).astype(BF16)
    last = mm(one_hot(iota((8, UNITS), 1) == UNITS - 1), w_input[2].astype(BF16))
    wx_mine[...] = mm_nt(last.astype(BF16), place)[0:1, :]
    for dx in range(1, 4):
        to = peer(0, 0, 4 - dx)
        for rows in (slice(0, 176), slice(256, 368), slice(384, 640)):
            send(w_mine.at[rows], w_all.at[dx, rows], send_sem.at[2], recv_x.at[1], to)
        send(wx_mine, wx_all.at[dx], send_sem.at[3], recv_x.at[2], to)
    w_all[0] = w_mine[...]
    wx_all[0] = wx_mine[...]

    for dy in range(4):
        first = 1 if dy == 0 else 0
        wait_bytes(req_recv.at[dy * 32 + first : dy * 32 + 8], recv_req.at[2 + dy])
    small[...] = jnp.zeros(small.shape, F32)
    for dy in range(4):
        small[8 * dy : 8 * dy + 8, :] = req_recv[dy * 32 : dy * 32 + 8].reshape(8, 128).astype(F32)
    asked = small[...].T.astype(I32)
    row_lane = iota((CAP, ROWS), 1)
    for dy in (2, 1, 3, 0):
        mask = jnp.concatenate(
            [
                one_hot(asked[0:CAP, 8 * dy + j : 8 * dy + j + 1] == row_lane)
                for j in range(8)
            ],
            axis=0,
        )
        rows = mm(mask, memb[...]).astype(BF16)
        for j in range(8):
            piece = rows[j * CAP : (j + 1) * CAP, :]
            if dy == 0 and j == 0:
                fetched[n] = piece
            else:
                row_send[dy * 8 + j] = piece
                back = (4 - j // 2) % 4 * 2 + j % 2
                send(
                    row_send.at[dy * 8 + j],
                    fetched.at[n],
                    send_sem.at[4],
                    recv_rows,
                    peer((4 - dy) % 4, back, 0),
                )

    for dy, dx, j in everyone:
        if dx != 0:
            to = peer(dy, j, dx)
            send(
                req_send.at[to[0]],
                req_recv.at[dy * 32 + dx * 8 + j],
                send_sem.at[0],
                recv_req.at[1],
                to,
            )

    vec[...] = jnp.zeros(vec.shape, F32)
    vec[0:1, 0:TIME] = frequency[...]
    vec[1:2, 0:TIME] = phase_shift[...]
    vec[2:3, 0:EMB] = b_merge[...]
    vec[3:4, 0:EMB] = b_out[...]
    vec[4:8, 0:UNITS] = gru_bias[...]
    freq = vec[0:1, 0:128]
    phase = vec[1:2, 0:128]

    wide_t[...] = jnp.zeros(wide_t.shape, F32)
    wide_t[0 : K + 2, :] = slot_ref[...].astype(F32)
    wide_t[16 : 16 + K, :] = nbr_gap[...].astype(F32)
    wide_t[32:33, :] = ev_time[...].astype(F32)
    cols[...] = wide_t[...].T
    end_cols[:, 0:EV] = slot_ref[0:1, :]
    end_cols[:, EV : 2 * EV] = slot_ref[1:2, :]

    for k in range(K):
        times[k] = cosine(cols[:, 16 + k : 17 + k] * freq + phase).astype(BF16)

    slot_lane = iota((128, SLOTS), 1)

    def mark(b, count):
        picks = cols[pl.ds(pl.multiple_of(b * 128, 128), 128), :].astype(I32)
        for k in range(K):
            hot[b, k * 128 : (k + 1) * 128, :] = one_hot(picks[:, 2 + k : 3 + k] == slot_lane)
        for e in range(2):
            mask = jnp.where(picks[:, e : e + 1] == slot_lane, 1.0, 0.0)
            count += jnp.sum(mask, axis=0, keepdims=True)
            ends[e, pl.ds(pl.multiple_of(b * 128, 128), 128), :] = mask.astype(BF16)
        return count

    hits[...] = lax.fori_loop(0, 4, mark, jnp.zeros((1, SLOTS), F32))

    r272 = iota((384, ATT), 0)
    c272 = iota((384, ATT), 1)
    place = one_hot(
        ((c272 < MEM) & (r272 == c272)) | ((c272 >= MEM) & (r272 == c272 + (256 - MEM)))
    )
    wkv[...] = jnp.zeros(wkv.shape, BF16)
    wkv[:, 0:ATT] = mm(place, w_key[...]).astype(BF16)
    wkv[:, 384 : 384 + ATT] = mm(place, w_value[...]).astype(BF16)
    wq[...] = jnp.zeros(wq.shape, BF16)
    wq[:, 0:ATT] = mm(place, w_query[...]).astype(BF16)
    r444 = iota((640, ATT + MEM), 0)
    c444 = iota((640, ATT + MEM), 1)
    place = one_hot(
        ((c444 < ATT) & (r444 == c444)) | ((c444 >= ATT) & (r444 == c444 + (384 - ATT)))
    )
    wm[...] = mm_nt(place, w_merge[...]).astype(BF16)

    widen = one_hot(iota((CAP, UNITS), 0) == iota((CAP, UNITS), 1))
    mem_b = memory[...].astype(BF16)
    gates = (
        w_input[0, :, 0:MEM] + w_hidden[0],
        w_input[1, :, 0:MEM] + w_hidden[1],
        w_input[2, :, 0:MEM],
        w_hidden[2],
    )
    for g, w in enumerate(gates):
        zed[g] = mm(mm(widen, w.astype(BF16)).astype(BF16), mem_b)
    own[...] = jnp.dot(
        jnp.where(
            (iota((CAP, MEM), 1) == iota((CAP, MEM), 0) + f * UNITS)
            & (iota((CAP, MEM), 0) < UNITS),
            1.0,
            0.0,
        ),
        memory[...],
        preferred_element_type=F32,
        precision=lax.Precision.HIGHEST,
    )

    wait_bytes(edge_recv.at[0:3], recv_x.at[0])
    edges = edge_recv[...].reshape(256, EV).astype(F32).T.astype(BF16)
    for e in range(2):
        msg[e * EV : (e + 1) * EV, 384:640] = edges
    ext_send[...] = jnp.zeros(ext_send.shape, F32)

    wait_bytes(fetched.at[0:31], recv_rows)
    table = fetched.reshape(SLOTS, 256)

    for e in range(2):
        src[e] = mm(ends[e], table[...])
    for e in range(2):
        msg[e * EV : (e + 1) * EV, 0:256] = src[1 - e].astype(BF16)
        stamp = src[e, :, MEM : MEM + 1] * 128.0 + src[e, :, MEM + 1 : MEM + 2]
        gap = cols[:, 32:33] - stamp
        msg[e * EV : (e + 1) * EV, 256:384] = cosine(gap * freq + phase).astype(BF16)

    wait_bytes(w_all.at[0:3, 0:544], recv_x.at[1])
    wait_bytes(wx_all.at[0:3], recv_x.at[2])
    rows4 = jnp.concatenate([wx_all[dx] for dx in range(4)] + [jnp.zeros((4, 640), F32)], axis=0)
    w_ext[...] = rows4.astype(BF16)

    for dy in (2, 1, 3, 0):
        base = at_y[dy] * CAP
        mask = one_hot(iota((384, 2 * EV), 0) + base == end_cols[...])
        sums = mm(mask, msg[...]).astype(BF16)
        for pair in range(2):
            w_pair = jnp.concatenate([w_all[2 * pair], w_all[2 * pair + 1]], axis=1)
            out = mm(sums, w_pair).astype(BF16)
            for i in range(2):
                main_send[dy, 2 * pair + i] = out[:, i * 128 : (i + 1) * 128].reshape(8, CAP, 128)
        ext_tmp[0:8, :] = mm_nt(w_ext[...], sums)
        ext_tmp[8:9, :] = hits[:, pl.ds(pl.multiple_of(base, 128), 384)]
        for j in range(8):
            count_row = ext_tmp[8:9, j * CAP : (j + 1) * CAP]
            for dx in range(4):
                ext_send[dy, dx, j, :, 0:CAP] = ext_tmp[dx : dx + 1, j * CAP : (j + 1) * CAP]
                ext_send[dy, dx, j, :, 64 : 64 + CAP] = count_row
        for j in range(8):
            for dx in range(4):
                if dy == 0 and dx == 0 and j == 0:
                    continue
                to = peer(dy, j, dx)
                send(
                    main_send.at[dy, dx, in_y[j]],
                    main_recv.at[dy, dx * 8 + j],
                    send_sem.at[5],
                    recv_main.at[dy],
                    to,
                )
                send(
                    ext_send.at[dy, dx, in_y[j]],
                    ext_recv.at[dy, dx * 8 + j],
                    send_sem.at[6],
                    recv_ext.at[dy],
                    to,
                )
    main_recv[0, 0] = main_send[0, 0, in_y[0]]
    ext_recv[0, 0] = ext_send[0, 0, in_y[0]]

    still = jnp.broadcast_to(cosine(phase), (EV, 128)).astype(BF16)
    query[...] = (
        mm(src[0].astype(BF16), wq[0:256, :]) + mm(still, wq[256:384, :])
    ) * (1.0 / math.sqrt(HEAD))
    lane_q = iota((16, 384), 1)
    first_head = lane_q < HEAD

    def attend(b, carry):
        at = pl.multiple_of(b * 128, 128)
        near[...] = mm(hot[b], table[...]).astype(BF16)
        code = times[:, pl.ds(at, 128), :].reshape(K * 128, 128)
        kv[...] = (mm(near[...], wkv[0:256, :]) + mm(code, wkv[256:384, :])).reshape(K, 128, 768)

        def group(g, inner):
            r = pl.multiple_of(g * 16, 16)
            q = query[pl.ds(at + r, 16), :]
            s0, s1 = [], []
            for k in range(K):
                t = q * kv[k, pl.ds(r, 16), 0:384]
                s0.append(jnp.sum(jnp.where(first_head, t, 0.0), axis=1, keepdims=True))
                s1.append(jnp.sum(jnp.where(first_head, 0.0, t), axis=1, keepdims=True))
            m0 = functools.reduce(jnp.maximum, s0)
            m1 = functools.reduce(jnp.maximum, s1)
            p0 = [jnp.exp(s - m0) for s in s0]
            p1 = [jnp.exp(s - m1) for s in s1]
            total = jnp.zeros((16, 384), F32)
            for k in range(K):
                w = jnp.where(first_head, p0[k], p1[k])
                total += w * kv[k, pl.ds(r, 16), 384:768]
            norm = jnp.where(first_head, sum(p0), sum(p1))
            att[pl.ds(at + r, 16), :] = (total / norm).astype(BF16)
            return inner

        lax.fori_loop(0, 8, group, 0)
        return carry

    lax.fori_loop(0, 4, attend, 0)
    hidden = mm(att[...], wm[0:384, :]) + mm(src[0].astype(BF16), wm[384:640, :])
    hidden = jnp.maximum(hidden + vec[2:3, 0:EMB], 0.0).astype(BF16)
    embedding[...] = (mm(hidden, w_out[...]) + vec[3:4, 0:EMB]).T.astype(BF16)

    wait_bytes(req_recv.at[0:96], recv_req.at[1])
    asked = req_recv[...].reshape(128, 128).astype(F32).T.astype(I32)
    for dy in (2, 1, 3, 0):
        for i in range(32):
            at = dy * 32 + i
            claims[i * CAP : (i + 1) * CAP, :] = one_hot(asked[0:CAP, at : at + 1] == row_lane)
        first = 1 if dy == 0 else 0
        wait_bytes(main_recv.at[dy, first:32], recv_main.at[dy])
        wait_bytes(ext_recv.at[dy, first:32], recv_ext.at[dy])
        for i in range(32):
            side[0:1, i * CAP : (i + 1) * CAP] = ext_recv[dy, i, :, 0:CAP]
            side[1:2, i * CAP : (i + 1) * CAP] = ext_recv[dy, i, :, 64 : 64 + CAP]
        count = side[1:2, :]
        high = jnp.floor(count * (1.0 / 128.0))
        row = iota((16, SLOTS), 0)
        rest = jnp.where(
            row == 0,
            side[0:1, :],
            jnp.where(row == 1, count - high * 128.0, jnp.where(row == 2, high, 0.0)),
        )
        left = jnp.concatenate(
            [main_recv[dy].reshape(SLOTS, 128).T, rest.astype(BF16)], axis=0
        )
        total = mm(left, claims[...])
        if dy == 2:
            acc[...] = total
        else:
            acc[...] += total

    small[...] = jnp.zeros(small.shape, F32)
    small[0:4, :] = vec[4:8, 0:128]
    bias = small[...].T
    b0, b1, b2, b3 = (bias[0:UNITS, g : g + 1] for g in range(4))
    heard = acc[129:130, :] + acc[130:131, :] * 128.0
    share = 1.0 / jnp.maximum(heard, 1.0)
    reset = jax.nn.sigmoid(acc[0:UNITS, :] * share + zed[0, 0:UNITS, :] + b0)
    update = jax.nn.sigmoid(acc[UNITS : 2 * UNITS, :] * share + zed[1, 0:UNITS, :] + b1)
    cand = jnp.tanh(
        acc[2 * UNITS : 3 * UNITS, :] * share
        + zed[2, 0:UNITS, :]
        + b2
        + reset * (zed[3, 0:UNITS, :] + b3)
    )
    mine = own[0:UNITS, :]
    fresh = (1.0 - update) * cand + update * mine
    new_memory[...] = jnp.where(heard > 0.0, fresh, mine)

    wait_bytes(req_recv.at[0:127], send_sem.at[0])
    wait_bytes(edge_recv.at[0:3], send_sem.at[1])
    wait_bytes(w_all.at[0:3, 0:544], send_sem.at[2])
    wait_bytes(wx_all.at[0:3], send_sem.at[3])
    wait_bytes(row_send.at[0:31], send_sem.at[4])
    wait_bytes(main_recv.at[0:3], send_sem.at[5])
    wait_bytes(main_recv.at[3, 0:31], send_sem.at[5])
    wait_bytes(ext_recv.at[0:3], send_sem.at[6])
    wait_bytes(ext_recv.at[3, 0:31], send_sem.at[6])


def step(
    memory,
    last_update,
    ev_time,
    nbr_gap,
    slot_rows,
    slot_ref,
    edge_feat,
    frequency,
    phase_shift,
    w_query,
    w_key,
    w_value,
    w_merge,
    b_merge,
    w_out,
    b_out,
    w_input,
    w_hidden,
    gru_bias,
):
    args = (
        memory.T,
        last_update.reshape(1, ROWS),
        ev_time.reshape(1, EV),
        nbr_gap.T,
        slot_rows,
        slot_ref.T,
        edge_feat.T,
        frequency.reshape(1, TIME),
        phase_shift.reshape(1, TIME),
        w_query,
        w_key,
        w_value,
        w_merge.T,
        b_merge.reshape(1, EMB),
        w_out,
        b_out.reshape(1, EMB),
        jnp.swapaxes(w_input, 1, 2),
        jnp.swapaxes(w_hidden, 1, 2),
        gru_bias,
    )
    vmem = pl.BlockSpec(memory_space=pltpu.VMEM)
    V, D = pltpu.VMEM, pltpu.SemaphoreType.DMA
    embedding, new_memory = pl.pallas_call(
        kernel,
        out_shape=(
            jax.ShapeDtypeStruct((EMB, EV), BF16),
            jax.ShapeDtypeStruct((UNITS, ROWS), F32),
        ),
        in_specs=[vmem] * len(args),
        out_specs=(vmem, vmem),
        scratch_shapes=[
            V((32, 1, 128), I32),
            V((128, 1, 128), I32),
            V((32, CAP, 256), BF16),
            V((32, CAP, 256), BF16),
            V((4, 64, EV), BF16),
            V((640, 128), BF16),
            V((1, 640), F32),
            V((4, 640, 128), BF16),
            V((4, 1, 640), F32),
            V((4, 4, 8, CAP, 128), BF16),
            V((4, 32, CAP, 128), BF16),
            V((4, 4, 8, 1, 128), F32),
            V((4, 32, 1, 128), F32),
            V((8, 256), F32),
            V((256, ROWS), F32),
            V((ROWS, 256), BF16),
            V((128, EV), F32),
            V((EV, 128), F32),
            V((128, 128), F32),
            V((K, EV, 128), BF16),
            V((384, 768), BF16),
            V((384, 384), BF16),
            V((640, EMB), BF16),
            V((8, 640), BF16),
            V((4, CAP, ROWS), F32),
            V((CAP, ROWS), F32),
            V((1, 2 * EV), I32),
            V((1, SLOTS), F32),
            V((2, EV, SLOTS), BF16),
            V((2, EV, 256), F32),
            V((2 * EV, 640), BF16),
            V((16, 384), F32),
            V((EV, 384), F32),
            V((4, K * 128, SLOTS), BF16),
            V((K * 128, 256), BF16),
            V((K, 128, 768), F32),
            V((EV, 384), BF16),
            V((SLOTS, ROWS), BF16),
            V((8, SLOTS), F32),
            V((144, ROWS), F32),
            D((7,)),
            D((6,)),
            D,
            D((3,)),
            D((4,)),
            D((4,)),
        ],
        compiler_params=pltpu.CompilerParams(
            collective_id=0, has_side_effects=True, vmem_limit_bytes=60 * 1024 * 1024
        ),
    )(*args)
    return embedding.T, new_memory.T


def solution(mesh):
    return jax.shard_map(
        step,
        mesh=mesh,
        in_specs=(
            P("node", None),
            P("node"),
            P(("node", "feat")),
            P(("node", "feat"), None),
            P(("node", "feat"), None),
            P(("node", "feat"), None),
            P("node", "feat"),
            P(),
            P(),
            P(),
            P(),
            P(),
            P(),
            P(),
            P(),
            P(),
            P(None, None, "feat"),
            P(None, None, "feat"),
            P(None, "feat"),
        ),
        out_specs=(P(("node", "feat"), None), P("node", "feat")),
        check_vma=False,
    )
```

time: 94.8 us -> 69.5 us (0.73)
  Pallas kernels: 80.5 us -> 66.3 us
  local copies, waits for them, and re-layouts: 13.3 us -> 2.33 us
    pallas_call x1, Pallas kernels: 80.5 us -> 66.3 us  [step(): pl.pallas_call(kernel, out_shape=(jax.ShapeDtypeStruct((EMB, EV), BF16),...]
    unnamed x15 -> x4, local copies, waits for them, and re-layouts: 9.65 us -> 2.33 us
    pallas_call x2 -> x0, local copies, waits for them, and re-layouts: 3.66 us -> none  [step(): pl.pallas_call(kernel, out_shape=(jax.ShapeDtypeStruct((EV, EMB), BF16),...]
where the time goes in v2:
time: 69.5 us; the launch traced here: 69.3 us
  Pallas kernels  66.3 us (95%)
  local copies, waits for them, and re-layouts  2.33 us (3%)
    pallas_call x1, Pallas kernels, step(): pl.pallas_call(kernel, out_shape=(jax.ShapeDtypeStruct((EMB, EV), BF16),...  66.3 us
    unnamed x4, local copies, waits for them, and re-layouts  2.33 us

profile of v2, /device:TPU:1, one launch (start us, length us, event | category | flops | bytes accessed | tf_op | source)
XLA Modules:
  0.0 69.3 jit_solution(6568353279995174657)
XLA Ops:
  0.6 66.3 %shard_map.194 = (bf16[172,512]{1,0:T(8,128)(2,1)}, f32[43,1024]{1,0:T(8,128)}) custom-call(f32[172,1024]{1,0:T(8,128)} %bitcast.15, s32[1,1024]{1,0:T(1,128)} %bitcast.24, s32[1,512]{1,0:T(1,128)} %bitcast.25, s32[10,512]{1,0:T(8,128)} %bitcast.22, s32[1,1536]{1,0:T(1,128)} %slot_rows.1, s32[12,512]{1,0:T(8,128)} %bitcast.23, bf16[64,2048]{1,0:T(8,128)(2,1)} %bitcast.17, ...), custom_call_target="tpu_custom_call" | custom-call | tf_op jit(solution)/shard_map/pallas_call | solution.py:543
  67.0 0.0 copy-start
  67.0 1.6 %copy.23 = bf16[512,172]{0,1:T(8,128)(2,1)} copy(bf16[512,172]{0,1:T(8,128)(2,1)} %bitcast.19) | data formatting | bytes 352256
  68.6 0.0 copy-done
  68.6 0.7 copy.24
Async XLA Ops:
  67.0 1.7 %copy-start = (f32[43,1024]{1,0:T(8,128)S(1)}, f32[43,1024]{1,0:T(8,128)}, u32[]{:S(2)}) copy-start(f32[43,1024]{1,0:T(8,128)} %get-tuple-element.5) | copy-start | bytes 528388

commit v3 on v2

--- a/solution.py
+++ b/solution.py
@@ -26,7 +26,21 @@
 MEM, TIME, ATT, EMB, UNITS = 172, 100, 272, 172, 43
 CAP, K, EV, ROWS, SLOTS = 48, 10, 512, 1024, 1536
 HEAD = ATT // 2
-GROUPS, PEERS = 4, 32
+
+HOME = (0, 0, 0, 0)
+
+
+def backward(way):
+    return tuple(3 if d == 2 else 0 for d in way[:3]) + (0,)
+
+
+RELAYED = {
+    way: backward(way)
+    for way in [
+        (dy, dz, dx, dc) for dy in range(4) for dz in range(4) for dx in range(4) for dc in range(2)
+    ]
+    if way[:3].count(2) >= 2 or way[:3] in ((2, 0, 0), (0, 2, 0), (0, 0, 2))
+}
 
 
 def cosine(x):
@@ -55,75 +69,89 @@
     return jnp.where(mask, 1.0, 0.0).astype(BF16)
 
 
-def kernel(
-    memory,
-    last_update,
-    ev_time,
-    nbr_gap,
-    slot_rows,
-    slot_ref,
-    edge_feat,
-    frequency,
-    phase_shift,
-    w_query,
-    w_key,
-    w_value,
-    w_merge,
-    b_merge,
-    w_out,
-    b_out,
-    w_input,
-    w_hidden,
-    gru_bias,
-    embedding,
-    new_memory,
-    req_send,
-    req_recv,
-    row_send,
-    fetched,
-    edge_recv,
-    w_mine,
-    wx_mine,
-    w_all,
-    wx_all,
-    main_send,
-    main_recv,
-    ext_send,
-    ext_recv,
-    vec,
-    mem_t,
-    memb,
-    wide_t,
-    cols,
-    small,
-    times,
-    wkv,
-    wq,
-    wm,
-    w_ext,
-    zed,
-    own,
-    end_cols,
-    hits,
-    ends,
-    src,
-    msg,
-    ext_tmp,
-    query,
-    hot,
-    near,
-    kv,
-    att,
-    claims,
-    side,
-    acc,
-    send_sem,
-    recv_req,
-    recv_rows,
-    recv_x,
-    recv_main,
-    recv_ext,
-):
+def kernel(*refs):
+    given, refs = refs[:19], refs[19:]
+    loaded, refs = refs[-19:], refs[:-19]
+    (
+        embedding,
+        new_memory,
+        req_send,
+        req_recv,
+        row_send,
+        fetched,
+        edge_recv,
+        w_mine,
+        wx_mine,
+        w_all,
+        wx_all,
+        main_send,
+        main_recv,
+        ext_send,
+        ext_recv,
+        relay_rows,
+        relay_main,
+        relay_ext,
+        vec,
+        mem_t,
+        memb,
+        wide_t,
+        cols,
+        small,
+        times,
+        wkv,
+        wq,
+        wm,
+        w_ext,
+        zed,
+        own,
+        end_cols,
+        hits,
+        ends,
+        src,
+        msg,
+        ext_tmp,
+        query,
+        hot,
+        near,
+        qk,
+        claims,
+        asked_by,
+        mix,
+        side,
+        acc,
+        send_sem,
+        recv_req,
+        recv_rows,
+        recv_x,
+        recv_main,
+        recv_ext,
+        recv_relay,
+        in_sem,
+    ) = refs
+    (
+        memory,
+        last_update,
+        ev_time,
+        nbr_gap,
+        slot_rows,
+        slot_ref,
+        edge_feat,
+        frequency,
+        phase_shift,
+        w_query,
+        w_key,
+        w_value,
+        w_merge,
+        b_merge,
+        w_out,
+        b_out,
+        w_input,
+        w_hidden,
+        gru_bias,
+    ) = loaded
+    loads = [
+        pltpu.make_async_copy(a, b, in_sem.at[i]) for i, (a, b) in enumerate(zip(given, loaded))
+    ]
     n = lax.axis_index("node")
     f = lax.axis_index("feat")
     y, z, c = n // 8, (n // 2) % 4, n % 2
@@ -149,6 +177,12 @@
     def wait_bytes(ref, sem):
         pltpu.make_async_copy(ref, ref, sem).wait()
 
+    def less(a, b):
+        return (a[0] - b[0]) % 4, (a[1] - b[1]) % 4, (a[2] - b[2]) % 4, (a[3] - b[3]) % 2
+
+    def there(d):
+        return peer(d[0], d[1] * 2 + d[3], d[2])
+
     everyone = [(dy, dx, j) for dy in range(4) for dx in range(4) for j in range(8)][1:]
 
     for dx in range(4):
@@ -156,17 +190,27 @@
         w_all[dx, 368:384, :] = jnp.zeros((16, 128), BF16)
 
     barrier = pltpu.get_barrier_semaphore()
-    for dy, dx, j in everyone:
+    near_by = [(dy, dx, j) for dy, dx, j in everyone if dx == 0 or (dy == 0 and j == 0)]
+    for dy, dx, j in near_by:
         pl.semaphore_signal(
             barrier, inc=1, device_id=peer(dy, j, dx), device_id_type=MESH
         )
+    for first in (4, 0, 1, 6):
+        loads[first].start()
+    for i in range(19):
+        if i not in (4, 0, 1, 6):
+            loads[i].start()
 
     req_send[...] = jnp.full(req_send.shape, -1, I32)
+    loads[4].wait()
     for o in range(32):
         req_send[o, :, 0:CAP] = slot_rows[:, o * CAP : (o + 1) * CAP]
     req_recv[0] = req_send[n]
+    loads[6].wait()
     edge_recv[f] = edge_feat[:, pl.ds(pl.multiple_of(f * EV, EV), EV)]
 
+    loads[0].wait()
+    loads[1].wait()
     mem_t[0:MEM, :] = memory[...]
     stamp = last_update[...].astype(F32)
     high = jnp.floor(stamp * (1.0 / 128.0))
@@ -176,7 +220,7 @@
     for b in range(4):
         memb[b * 256 : (b + 1) * 256, :] = mem_t[:, b * 256 : (b + 1) * 256].T.astype(BF16)
 
-    pl.semaphore_wait(barrier, 127)
+    pl.semaphore_wait(barrier, len(near_by))
 
     for dy, dx, j in everyone:
         if dx == 0:
@@ -198,6 +242,7 @@
             to,
         )
 
+    loads[16].wait()
     r640 = iota((640, 700), 0)
     c640 = iota((640, 700), 1)
     place = one_hot(
@@ -229,7 +274,8 @@
         small[8 * dy : 8 * dy + 8, :] = req_recv[dy * 32 : dy * 32 + 8].reshape(8, 128).astype(F32)
     asked = small[...].T.astype(I32)
     row_lane = iota((CAP, ROWS), 1)
-    for dy in (2, 1, 3, 0):
+    row_relays = []
+    for dy in (2, 0, 1, 3):
         mask = jnp.concatenate(
             [
                 one_hot(asked[0:CAP, 8 * dy + j : 8 * dy + j + 1] == row_lane)
@@ -239,20 +285,35 @@
         )
         rows = mm(mask, memb[...]).astype(BF16)
         for j in range(8):
-            piece = rows[j * CAP : (j + 1) * CAP, :]
             if dy == 0 and j == 0:
-                fetched[n] = piece
+                fetched[n] = rows[0:CAP, :]
             else:
-                row_send[dy * 8 + j] = piece
-                back = (4 - j // 2) % 4 * 2 + j % 2
-                send(
-                    row_send.at[dy * 8 + j],
-                    fetched.at[n],
-                    send_sem.at[4],
-                    recv_rows,
-                    peer((4 - dy) % 4, back, 0),
-                )
-
+                row_send[dy * 8 + j] = rows[j * CAP : (j + 1) * CAP, :]
+        for j in (4, 5, 2, 3, 6, 7, 1, 0):
+            if dy == 0 and j == 0:
+                continue
+            way = less(HOME, (dy, j // 2, 0, j % 2))
+            step = RELAYED.get(way)
+            if step is None:
+                dst, sem, to = fetched.at[n], recv_rows, there(way)
+            else:
+                dst, sem, to = relay_rows.at[len(row_relays)], recv_relay.at[0], there(step)
+                row_relays.append((way, step))
+            send(row_send.at[dy * 8 + j], dst, send_sem.at[4], sem, to)
+
+    def pass_rows():
+        wait_bytes(relay_rows, recv_relay.at[0])
+        for at, (way, step) in enumerate(row_relays):
+            origin = there(less(HOME, step))[0]
+            send(
+                relay_rows.at[at],
+                fetched.at[origin],
+                send_sem.at[4],
+                recv_rows,
+                there(less(way, step)),
+            )
+
+    wait_bytes(edge_recv.at[0:3], recv_x.at[0])
     for dy, dx, j in everyone:
         if dx != 0:
             to = peer(dy, j, dx)
@@ -264,6 +325,8 @@
                 to,
             )
 
+    for i in (2, 3, 5, 7, 8, 9, 10, 11, 12, 13, 14, 15, 17, 18):
+        loads[i].wait()
     vec[...] = jnp.zeros(vec.shape, F32)
     vec[0:1, 0:TIME] = frequency[...]
     vec[1:2, 0:TIME] = phase_shift[...]
@@ -273,6 +336,8 @@
     freq = vec[0:1, 0:128]
     phase = vec[1:2, 0:128]
 
+    pass_rows()
+
     wide_t[...] = jnp.zeros(wide_t.shape, F32)
     wide_t[0 : K + 2, :] = slot_ref[...].astype(F32)
     wide_t[16 : 16 + K, :] = nbr_gap[...].astype(F32)
@@ -282,7 +347,7 @@
     end_cols[:, EV : 2 * EV] = slot_ref[1:2, :]
 
     for k in range(K):
-        times[k] = cosine(cols[:, 16 + k : 17 + k] * freq + phase).astype(BF16)
+        times[k] = cosine(cols[:, 16 + k : 17 + k] * freq + phase).astype(BF16).astype(F32)
 
     slot_lane = iota((128, SLOTS), 1)
 
@@ -337,7 +402,6 @@
         precision=lax.Precision.HIGHEST,
     )
 
-    wait_bytes(edge_recv.at[0:3], recv_x.at[0])
     edges = edge_recv[...].reshape(256, EV).astype(F32).T.astype(BF16)
     for e in range(2):
         msg[e * EV : (e + 1) * EV, 384:640] = edges
@@ -359,7 +423,8 @@
     rows4 = jnp.concatenate([wx_all[dx] for dx in range(4)] + [jnp.zeros((4, 640), F32)], axis=0)
     w_ext[...] = rows4.astype(BF16)
 
-    for dy in (2, 1, 3, 0):
+    relays = [[], []]
+    for dy in (2, 0, 1, 3):
         base = at_y[dy] * CAP
         mask = one_hot(iota((384, 2 * EV), 0) + base == end_cols[...])
         sums = mm(mask, msg[...]).astype(BF16)
@@ -375,25 +440,49 @@
             for dx in range(4):
                 ext_send[dy, dx, j, :, 0:CAP] = ext_tmp[dx : dx + 1, j * CAP : (j + 1) * CAP]
                 ext_send[dy, dx, j, :, 64 : 64 + CAP] = count_row
-        for j in range(8):
-            for dx in range(4):
-                if dy == 0 and dx == 0 and j == 0:
-                    continue
-                to = peer(dy, j, dx)
-                send(
-                    main_send.at[dy, dx, in_y[j]],
-                    main_recv.at[dy, dx * 8 + j],
-                    send_sem.at[5],
-                    recv_main.at[dy],
-                    to,
-                )
-                send(
-                    ext_send.at[dy, dx, in_y[j]],
-                    ext_recv.at[dy, dx * 8 + j],
-                    send_sem.at[6],
-                    recv_ext.at[dy],
-                    to,
-                )
+        batch = 0 if dy == 2 else 1
+        ways = [(dy, j // 2, dx, j % 2) for j in range(8) for dx in range(4)]
+        ways = sorted(ways, key=lambda way: way not in RELAYED)
+        for way in ways:
+            if way == HOME:
+                continue
+            dx, j = way[2], way[1] * 2 + way[3]
+            step = RELAYED.get(way)
+            if step is None:
+                to = there(way)
+                to_main, to_ext = main_recv.at[dy, dx * 8 + j], ext_recv.at[dy, dx * 8 + j]
+                main_sem, ext_sem = recv_main.at[dy], recv_ext.at[dy]
+            else:
+                to = there(step)
+                at = 16 * batch + len(relays[batch])
+                to_main, to_ext = relay_main.at[at], relay_ext.at[at]
+                main_sem, ext_sem = recv_relay.at[1 + 2 * batch], recv_relay.at[2 + 2 * batch]
+                relays[batch].append((at, way, step))
+            send(main_send.at[dy, dx, in_y[j]], to_main, send_sem.at[5], main_sem, to)
+            send(ext_send.at[dy, dx, in_y[j]], to_ext, send_sem.at[6], ext_sem, to)
+
+    def pass_sums(batch):
+        first, end = (0, 16) if batch == 0 else (16, 26)
+        wait_bytes(relay_main.at[first:end], recv_relay.at[1 + 2 * batch])
+        wait_bytes(relay_ext.at[first:end], recv_relay.at[2 + 2 * batch])
+        for at, way, step in relays[batch]:
+            to = there(less(way, step))
+            dy, dx, j = way[0], way[2], way[1] * 2 + way[3]
+            send(
+                relay_main.at[at],
+                main_recv.at[dy, dx * 8 + j],
+                send_sem.at[5],
+                recv_main.at[dy],
+                to,
+            )
+            send(
+                relay_ext.at[at],
+                ext_recv.at[dy, dx * 8 + j],
+                send_sem.at[6],
+                recv_ext.at[dy],
+                to,
+            )
+
     main_recv[0, 0] = main_send[0, 0, in_y[0]]
     ext_recv[0, 0] = ext_send[0, 0, in_y[0]]
 
@@ -401,49 +490,83 @@
     query[...] = (
         mm(src[0].astype(BF16), wq[0:256, :]) + mm(still, wq[256:384, :])
     ) * (1.0 / math.sqrt(HEAD))
-    lane_q = iota((16, 384), 1)
-    first_head = lane_q < HEAD
+    head_of = iota((EV, 384), 1) < HEAD
+    for h in range(2):
+        part = query[...]
+        part = jnp.where(head_of, part, 0.0) if h == 0 else jnp.where(head_of, 0.0, part)
+        coarse = part.astype(BF16)
+        fine = (part - coarse.astype(F32)).astype(BF16)
+        qk[h] = mm_nt(coarse, wkv[:, 0:384]) + mm_nt(fine, wkv[:, 0:384])
+    pass_sums(0)
+
+    wait_bytes(req_recv.at[0:96], recv_req.at[1])
+    for dy in range(4):
+        small[...] = jnp.zeros(small.shape, F32)
+        small[0:32, :] = req_recv[dy * 32 : dy * 32 + 32].reshape(32, 128).astype(F32)
+        asked_by[dy] = small[...].T
 
     def attend(b, carry):
         at = pl.multiple_of(b * 128, 128)
-        near[...] = mm(hot[b], table[...]).astype(BF16)
-        code = times[:, pl.ds(at, 128), :].reshape(K * 128, 128)
-        kv[...] = (mm(near[...], wkv[0:256, :]) + mm(code, wkv[256:384, :])).reshape(K, 128, 768)
+        near[...] = mm(hot[b], table[...]).reshape(K, 128, 256)
 
         def group(g, inner):
             r = pl.multiple_of(g * 16, 16)
-            q = query[pl.ds(at + r, 16), :]
+            rows = pl.ds(at + r, 16)
+            q0, q1 = qk[0, rows, :], qk[1, rows, :]
             s0, s1 = [], []
             for k in range(K):
-                t = q * kv[k, pl.ds(r, 16), 0:384]
-                s0.append(jnp.sum(jnp.where(first_head, t, 0.0), axis=1, keepdims=True))
-                s1.append(jnp.sum(jnp.where(first_head, 0.0, t), axis=1, keepdims=True))
+                x, t = near[k, pl.ds(r, 16), :], times[k, rows, :]
+                u0 = x * q0[:, 0:256]
+                u1 = x * q1[:, 0:256]
+                u0 = u0[:, 0:128] + u0[:, 128:256] + t * q0[:, 256:384]
+                u1 = u1[:, 0:128] + u1[:, 128:256] + t * q1[:, 256:384]
+                s0.append(jnp.sum(u0, axis=1, keepdims=True))
+                s1.append(jnp.sum(u1, axis=1, keepdims=True))
             m0 = functools.reduce(jnp.maximum, s0)
             m1 = functools.reduce(jnp.maximum, s1)
             p0 = [jnp.exp(s - m0) for s in s0]
             p1 = [jnp.exp(s - m1) for s in s1]
-            total = jnp.zeros((16, 384), F32)
+            n0 = 1.0 / sum(p0)
+            n1 = 1.0 / sum(p1)
+            a0 = a1 = jnp.zeros((16, 256), F32)
+            c0 = c1 = jnp.zeros((16, 128), F32)
             for k in range(K):
-                w = jnp.where(first_head, p0[k], p1[k])
-                total += w * kv[k, pl.ds(r, 16), 384:768]
-            norm = jnp.where(first_head, sum(p0), sum(p1))
-            att[pl.ds(at + r, 16), :] = (total / norm).astype(BF16)
+                x, t = near[k, pl.ds(r, 16), :], times[k, rows, :]
+                a0 += p0[k] * x
+                a1 += p1[k] * x
+                c0 += p0[k] * t
+                c1 += p1[k] * t
+            mix[0, rows, 0:256] = a0 * n0
+            mix[1, rows, 0:256] = a1 * n1
+            mix[0, rows, 256:384] = c0 * n0
+            mix[1, rows, 256:384] = c1 * n1
             return inner
 
         lax.fori_loop(0, 8, group, 0)
+        for i in range(32):
+            claims[b, i * CAP : (i + 1) * CAP, :] = one_hot(
+                asked_by[b, 0:CAP, i : i + 1].astype(I32) == row_lane
+            )
+
+        @pl.when(b == 1)
+        def _():
+            pass_sums(1)
+
         return carry
 
     lax.fori_loop(0, 4, attend, 0)
-    hidden = mm(att[...], wm[0:384, :]) + mm(src[0].astype(BF16), wm[384:640, :])
+    halves = []
+    for h in range(2):
+        part = mix[h]
+        coarse = part.astype(BF16)
+        fine = (part - coarse.astype(F32)).astype(BF16)
+        halves.append(mm(coarse, wkv[:, 384:768]) + mm(fine, wkv[:, 384:768]))
+    attended = jnp.where(head_of, halves[0], halves[1]).astype(BF16)
+    hidden = mm(attended, wm[0:384, :]) + mm(src[0].astype(BF16), wm[384:640, :])
     hidden = jnp.maximum(hidden + vec[2:3, 0:EMB], 0.0).astype(BF16)
     embedding[...] = (mm(hidden, w_out[...]) + vec[3:4, 0:EMB]).T.astype(BF16)
 
-    wait_bytes(req_recv.at[0:96], recv_req.at[1])
-    asked = req_recv[...].reshape(128, 128).astype(F32).T.astype(I32)
-    for dy in (2, 1, 3, 0):
-        for i in range(32):
-            at = dy * 32 + i
-            claims[i * CAP : (i + 1) * CAP, :] = one_hot(asked[0:CAP, at : at + 1] == row_lane)
+    for dy in (2, 0, 1, 3):
         first = 1 if dy == 0 else 0
         wait_bytes(main_recv.at[dy, first:32], recv_main.at[dy])
         wait_bytes(ext_recv.at[dy, first:32], recv_ext.at[dy])
@@ -461,7 +584,7 @@
         left = jnp.concatenate(
             [main_recv[dy].reshape(SLOTS, 128).T, rest.astype(BF16)], axis=0
         )
-        total = mm(left, claims[...])
+        total = mm(left, claims[dy])
         if dy == 2:
             acc[...] = total
         else:
@@ -490,10 +613,13 @@
     wait_bytes(w_all.at[0:3, 0:544], send_sem.at[2])
     wait_bytes(wx_all.at[0:3], send_sem.at[3])
     wait_bytes(row_send.at[0:31], send_sem.at[4])
+    wait_bytes(relay_rows, send_sem.at[4])
     wait_bytes(main_recv.at[0:3], send_sem.at[5])
     wait_bytes(main_recv.at[3, 0:31], send_sem.at[5])
+    wait_bytes(relay_main, send_sem.at[5])
     wait_bytes(ext_recv.at[0:3], send_sem.at[6])
     wait_bytes(ext_recv.at[3, 0:31], send_sem.at[6])
+    wait_bytes(relay_ext, send_sem.at[6])
 
 
 def step(
@@ -546,7 +672,7 @@
             jax.ShapeDtypeStruct((EMB, EV), BF16),
             jax.ShapeDtypeStruct((UNITS, ROWS), F32),
         ),
-        in_specs=[vmem] * len(args),
+        in_specs=[pl.BlockSpec(memory_space=pl.ANY)] * len(args),
         out_specs=(vmem, vmem),
         scratch_shapes=[
             V((32, 1, 128), I32),
@@ -562,13 +688,16 @@
             V((4, 32, CAP, 128), BF16),
             V((4, 4, 8, 1, 128), F32),
             V((4, 32, 1, 128), F32),
+            V((6, CAP, 256), BF16),
+            V((26, CAP, 128), BF16),
+            V((26, 1, 128), F32),
             V((8, 256), F32),
             V((256, ROWS), F32),
             V((ROWS, 256), BF16),
             V((128, EV), F32),
             V((EV, 128), F32),
             V((128, 128), F32),
-            V((K, EV, 128), BF16),
+            V((K, EV, 128), F32),
             V((384, 768), BF16),
             V((384, 384), BF16),
             V((640, EMB), BF16),
@@ -583,10 +712,11 @@
             V((16, 384), F32),
             V((EV, 384), F32),
             V((4, K * 128, SLOTS), BF16),
-            V((K * 128, 256), BF16),
-            V((K, 128, 768), F32),
-            V((EV, 384), BF16),
-            V((SLOTS, ROWS), BF16),
+            V((K, 128, 256), F32),
+            V((2, EV, 384), F32),
+            V((4, SLOTS, ROWS), BF16),
+            V((4, 128, 128), F32),
+            V((2, EV, 384), F32),
             V((8, SLOTS), F32),
             V((144, ROWS), F32),
             D((7,)),
@@ -595,7 +725,10 @@
             D((3,)),
             D((4,)),
             D((4,)),
-        ],
+            D((5,)),
+            D((19,)),
+        ]
+        + [V(a.shape, a.dtype) for a in args],
         compiler_params=pltpu.CompilerParams(
             collective_id=0, has_side_effects=True, vmem_limit_bytes=60 * 1024 * 1024
         ),

time: 69.5 us -> 77.2 us (1.11)
  the two profiles are of different devices: /device:TPU:1 before, /device:TPU:6 now
where the time goes in v3:
time: 77.2 us; the launch traced here: 77 us
  Pallas kernels  74 us (96%)
  local copies, waits for them, and re-layouts  2.33 us (3%)
    pallas_call x1, Pallas kernels, step(): pl.pallas_call(kernel, out_shape=(jax.ShapeDtypeStruct((EMB, EV), BF16),...  74 us
    unnamed x4, local copies, waits for them, and re-layouts  2.33 us

profile of v3, /device:TPU:6, one launch (start us, length us, event | category | flops | bytes accessed | tf_op | source)
XLA Modules:
  0.0 77.0 jit_solution(15927940826221237456)
XLA Ops:
  0.6 74.0 %shard_map.194 = (bf16[172,512]{1,0:T(8,128)(2,1)}, f32[43,1024]{1,0:T(8,128)}) custom-call(f32[172,1024]{1,0:T(8,128)} %bitcast.15, s32[1,1024]{1,0:T(1,128)} %bitcast.24, s32[1,512]{1,0:T(1,128)} %bitcast.25, s32[10,512]{1,0:T(8,128)} %bitcast.22, s32[1,1536]{1,0:T(1,128)} %refs_4_.1, s32[12,512]{1,0:T(8,128)} %bitcast.23, bf16[64,2048]{1,0:T(8,128)(2,1)} %bitcast.17, ...), custom_call_target="tpu_custom_call" | custom-call | tf_op jit(solution)/shard_map/pallas_call | solution.py:669
  74.7 0.0 copy-start
  74.7 1.6 %copy.23 = bf16[512,172]{0,1:T(8,128)(2,1)} copy(bf16[512,172]{0,1:T(8,128)(2,1)} %bitcast.19) | data formatting | bytes 352256
  76.3 0.0 copy-done
  76.3 0.7 copy.24
Async XLA Ops:
  74.7 1.7 %copy-start = (f32[43,1024]{1,0:T(8,128)S(1)}, f32[43,1024]{1,0:T(8,128)}, u32[]{:S(2)}) copy-start(f32[43,1024]{1,0:T(8,128)} %get-tuple-element.5) | copy-start | bytes 528388

commit v4 on v3

--- a/solution.py
+++ b/solution.py
@@ -26,21 +26,6 @@
 MEM, TIME, ATT, EMB, UNITS = 172, 100, 272, 172, 43
 CAP, K, EV, ROWS, SLOTS = 48, 10, 512, 1024, 1536
 HEAD = ATT // 2
-
-HOME = (0, 0, 0, 0)
-
-
-def backward(way):
-    return tuple(3 if d == 2 else 0 for d in way[:3]) + (0,)
-
-
-RELAYED = {
-    way: backward(way)
-    for way in [
-        (dy, dz, dx, dc) for dy in range(4) for dz in range(4) for dx in range(4) for dc in range(2)
-    ]
-    if way[:3].count(2) >= 2 or way[:3] in ((2, 0, 0), (0, 2, 0), (0, 0, 2))
-}
 
 
 def cosine(x):
@@ -88,9 +73,6 @@
         main_recv,
         ext_send,
         ext_recv,
-        relay_rows,
-        relay_main,
-        relay_ext,
         vec,
         mem_t,
         memb,
@@ -125,7 +107,6 @@
         recv_x,
         recv_main,
         recv_ext,
-        recv_relay,
         in_sem,
     ) = refs
     (
@@ -177,12 +158,6 @@
     def wait_bytes(ref, sem):
         pltpu.make_async_copy(ref, ref, sem).wait()
 
-    def less(a, b):
-        return (a[0] - b[0]) % 4, (a[1] - b[1]) % 4, (a[2] - b[2]) % 4, (a[3] - b[3]) % 2
-
-    def there(d):
-        return peer(d[0], d[1] * 2 + d[3], d[2])
-
     everyone = [(dy, dx, j) for dy in range(4) for dx in range(4) for j in range(8)][1:]
 
     for dx in range(4):
@@ -266,6 +241,28 @@
     w_all[0] = w_mine[...]
     wx_all[0] = wx_mine[...]
 
+    for i in (2, 3, 5, 7, 8, 9, 10, 11, 12, 13, 14, 15, 17, 18):
+        loads[i].wait()
+    vec[...] = jnp.zeros(vec.shape, F32)
+    vec[0:1, 0:TIME] = frequency[...]
+    vec[1:2, 0:TIME] = phase_shift[...]
+    vec[2:3, 0:EMB] = b_merge[...]
+    vec[3:4, 0:EMB] = b_out[...]
+    vec[4:8, 0:UNITS] = gru_bias[...]
+    freq = vec[0:1, 0:128]
+    phase = vec[1:2, 0:128]
+
+    wide_t[...] = jnp.zeros(wide_t.shape, F32)
+    wide_t[0 : K + 2, :] = slot_ref[...].astype(F32)
+    wide_t[16 : 16 + K, :] = nbr_gap[...].astype(F32)
+    wide_t[32:33, :] = ev_time[...].astype(F32)
+    cols[...] = wide_t[...].T
+    end_cols[:, 0:EV] = slot_ref[0:1, :]
+    end_cols[:, EV : 2 * EV] = slot_ref[1:2, :]
+
+    for k in range(K):
+        times[k] = cosine(cols[:, 16 + k : 17 + k] * freq + phase).astype(BF16).astype(F32)
+
     for dy in range(4):
         first = 1 if dy == 0 else 0
         wait_bytes(req_recv.at[dy * 32 + first : dy * 32 + 8], recv_req.at[2 + dy])
@@ -274,8 +271,7 @@
         small[8 * dy : 8 * dy + 8, :] = req_recv[dy * 32 : dy * 32 + 8].reshape(8, 128).astype(F32)
     asked = small[...].T.astype(I32)
     row_lane = iota((CAP, ROWS), 1)
-    row_relays = []
-    for dy in (2, 0, 1, 3):
+    for dy in (2, 1, 3, 0):
         mask = jnp.concatenate(
             [
                 one_hot(asked[0:CAP, 8 * dy + j : 8 * dy + j + 1] == row_lane)
@@ -292,25 +288,13 @@
         for j in (4, 5, 2, 3, 6, 7, 1, 0):
             if dy == 0 and j == 0:
                 continue
-            way = less(HOME, (dy, j // 2, 0, j % 2))
-            step = RELAYED.get(way)
-            if step is None:
-                dst, sem, to = fetched.at[n], recv_rows, there(way)
-            else:
-                dst, sem, to = relay_rows.at[len(row_relays)], recv_relay.at[0], there(step)
-                row_relays.append((way, step))
-            send(row_send.at[dy * 8 + j], dst, send_sem.at[4], sem, to)
-
-    def pass_rows():
-        wait_bytes(relay_rows, recv_relay.at[0])
-        for at, (way, step) in enumerate(row_relays):
-            origin = there(less(HOME, step))[0]
+            back = (4 - j // 2) % 4 * 2 + j % 2
             send(
-                relay_rows.at[at],
-                fetched.at[origin],
+                row_send.at[dy * 8 + j],
+                fetched.at[n],
                 send_sem.at[4],
-                recv_rows,
-                there(less(way, step)),
+                recv_rows.at[dy],
+                peer((4 - dy) % 4, back, 0),
             )
 
     wait_bytes(edge_recv.at[0:3], recv_x.at[0])
@@ -324,30 +308,6 @@
                 recv_req.at[1],
                 to,
             )
-
-    for i in (2, 3, 5, 7, 8, 9, 10, 11, 12, 13, 14, 15, 17, 18):
-        loads[i].wait()
-    vec[...] = jnp.zeros(vec.shape, F32)
-    vec[0:1, 0:TIME] = frequency[...]
-    vec[1:2, 0:TIME] = phase_shift[...]
-    vec[2:3, 0:EMB] = b_merge[...]
-    vec[3:4, 0:EMB] = b_out[...]
-    vec[4:8, 0:UNITS] = gru_bias[...]
-    freq = vec[0:1, 0:128]
-    phase = vec[1:2, 0:128]
-
-    pass_rows()
-
-    wide_t[...] = jnp.zeros(wide_t.shape, F32)
-    wide_t[0 : K + 2, :] = slot_ref[...].astype(F32)
-    wide_t[16 : 16 + K, :] = nbr_gap[...].astype(F32)
-    wide_t[32:33, :] = ev_time[...].astype(F32)
-    cols[...] = wide_t[...].T
-    end_cols[:, 0:EV] = slot_ref[0:1, :]
-    end_cols[:, EV : 2 * EV] = slot_ref[1:2, :]
-
-    for k in range(K):
-        times[k] = cosine(cols[:, 16 + k : 17 + k] * freq + phase).astype(BF16).astype(F32)
 
     slot_lane = iota((128, SLOTS), 1)
 
@@ -407,11 +367,36 @@
         msg[e * EV : (e + 1) * EV, 384:640] = edges
     ext_send[...] = jnp.zeros(ext_send.shape, F32)
 
-    wait_bytes(fetched.at[0:31], recv_rows)
-    table = fetched.reshape(SLOTS, 256)
-
+    def half_of(table_of, lanes_of, half):
+        return (
+            jnp.concatenate([table_of(dy) for dy in half], axis=0),
+            lambda ref: jnp.concatenate([lanes_of(ref, dy) for dy in half], axis=1),
+        )
+
+    def owners(dy):
+        return fetched[pl.ds(at_y[dy], 8)].reshape(384, 256)
+
+    def marks(view, dy):
+        return view[:, pl.ds(pl.multiple_of(at_y[dy] * CAP, 128), 384)]
+
+    for dy in (1, 2):
+        wait_bytes(fetched.at[0:8], recv_rows.at[dy])
+    table, lanes = half_of(owners, marks, (1, 2))
     for e in range(2):
-        src[e] = mm(ends[e], table[...])
+        src[e] = mm(lanes(ends.at[e]), table)
+
+    def first_half(b, carry):
+        table, lanes = half_of(owners, marks, (1, 2))
+        near[b] = mm(lanes(hot.at[b]), table).reshape(K, 128, 256)
+        return carry
+
+    lax.fori_loop(0, 4, first_half, 0)
+
+    wait_bytes(fetched.at[0:8], recv_rows.at[3])
+    wait_bytes(fetched.at[0:7], recv_rows.at[0])
+    table, lanes = half_of(owners, marks, (3, 0))
+    for e in range(2):
+        src[e] += mm(lanes(ends.at[e]), table)
     for e in range(2):
         msg[e * EV : (e + 1) * EV, 0:256] = src[1 - e].astype(BF16)
         stamp = src[e, :, MEM : MEM + 1] * 128.0 + src[e, :, MEM + 1 : MEM + 2]
@@ -423,8 +408,7 @@
     rows4 = jnp.concatenate([wx_all[dx] for dx in range(4)] + [jnp.zeros((4, 640), F32)], axis=0)
     w_ext[...] = rows4.astype(BF16)
 
-    relays = [[], []]
-    for dy in (2, 0, 1, 3):
+    for dy in (2, 1, 3, 0):
         base = at_y[dy] * CAP
         mask = one_hot(iota((384, 2 * EV), 0) + base == end_cols[...])
         sums = mm(mask, msg[...]).astype(BF16)
@@ -440,49 +424,25 @@
             for dx in range(4):
                 ext_send[dy, dx, j, :, 0:CAP] = ext_tmp[dx : dx + 1, j * CAP : (j + 1) * CAP]
                 ext_send[dy, dx, j, :, 64 : 64 + CAP] = count_row
-        batch = 0 if dy == 2 else 1
-        ways = [(dy, j // 2, dx, j % 2) for j in range(8) for dx in range(4)]
-        ways = sorted(ways, key=lambda way: way not in RELAYED)
-        for way in ways:
-            if way == HOME:
-                continue
-            dx, j = way[2], way[1] * 2 + way[3]
-            step = RELAYED.get(way)
-            if step is None:
-                to = there(way)
-                to_main, to_ext = main_recv.at[dy, dx * 8 + j], ext_recv.at[dy, dx * 8 + j]
-                main_sem, ext_sem = recv_main.at[dy], recv_ext.at[dy]
-            else:
-                to = there(step)
-                at = 16 * batch + len(relays[batch])
-                to_main, to_ext = relay_main.at[at], relay_ext.at[at]
-                main_sem, ext_sem = recv_relay.at[1 + 2 * batch], recv_relay.at[2 + 2 * batch]
-                relays[batch].append((at, way, step))
-            send(main_send.at[dy, dx, in_y[j]], to_main, send_sem.at[5], main_sem, to)
-            send(ext_send.at[dy, dx, in_y[j]], to_ext, send_sem.at[6], ext_sem, to)
-
-    def pass_sums(batch):
-        first, end = (0, 16) if batch == 0 else (16, 26)
-        wait_bytes(relay_main.at[first:end], recv_relay.at[1 + 2 * batch])
-        wait_bytes(relay_ext.at[first:end], recv_relay.at[2 + 2 * batch])
-        for at, way, step in relays[batch]:
-            to = there(less(way, step))
-            dy, dx, j = way[0], way[2], way[1] * 2 + way[3]
-            send(
-                relay_main.at[at],
-                main_recv.at[dy, dx * 8 + j],
-                send_sem.at[5],
-                recv_main.at[dy],
-                to,
-            )
-            send(
-                relay_ext.at[at],
-                ext_recv.at[dy, dx * 8 + j],
-                send_sem.at[6],
-                recv_ext.at[dy],
-                to,
-            )
-
+        for j in range(8):
+            for dx in range(4):
+                if dy == 0 and dx == 0 and j == 0:
+                    continue
+                to = peer(dy, j, dx)
+                send(
+                    main_send.at[dy, dx, in_y[j]],
+                    main_recv.at[dy, dx * 8 + j],
+                    send_sem.at[5],
+                    recv_main.at[dy],
+                    to,
+                )
+                send(
+                    ext_send.at[dy, dx, in_y[j]],
+                    ext_recv.at[dy, dx * 8 + j],
+                    send_sem.at[6],
+                    recv_ext.at[dy],
+                    to,
+                )
     main_recv[0, 0] = main_send[0, 0, in_y[0]]
     ext_recv[0, 0] = ext_send[0, 0, in_y[0]]
 
@@ -497,7 +457,6 @@
         coarse = part.astype(BF16)
         fine = (part - coarse.astype(F32)).astype(BF16)
         qk[h] = mm_nt(coarse, wkv[:, 0:384]) + mm_nt(fine, wkv[:, 0:384])
-    pass_sums(0)
 
     wait_bytes(req_recv.at[0:96], recv_req.at[1])
     for dy in range(4):
@@ -507,7 +466,8 @@
 
     def attend(b, carry):
         at = pl.multiple_of(b * 128, 128)
-        near[...] = mm(hot[b], table[...]).reshape(K, 128, 256)
+        table, lanes = half_of(owners, marks, (3, 0))
+        near[b] += mm(lanes(hot.at[b]), table).reshape(K, 128, 256)
 
         def group(g, inner):
             r = pl.multiple_of(g * 16, 16)
@@ -515,7 +475,7 @@
             q0, q1 = qk[0, rows, :], qk[1, rows, :]
             s0, s1 = [], []
             for k in range(K):
-                x, t = near[k, pl.ds(r, 16), :], times[k, rows, :]
+                x, t = near[b, k, pl.ds(r, 16), :], times[k, rows, :]
                 u0 = x * q0[:, 0:256]
                 u1 = x * q1[:, 0:256]
                 u0 = u0[:, 0:128] + u0[:, 128:256] + t * q0[:, 256:384]
@@ -531,7 +491,7 @@
             a0 = a1 = jnp.zeros((16, 256), F32)
             c0 = c1 = jnp.zeros((16, 128), F32)
             for k in range(K):
-                x, t = near[k, pl.ds(r, 16), :], times[k, rows, :]
+                x, t = near[b, k, pl.ds(r, 16), :], times[k, rows, :]
                 a0 += p0[k] * x
                 a1 += p1[k] * x
                 c0 += p0[k] * t
@@ -542,15 +502,11 @@
             mix[1, rows, 256:384] = c1 * n1
             return inner
 
-        lax.fori_loop(0, 8, group, 0)
+        lax.fori_loop(0, 8, group, 0, unroll=2)
         for i in range(32):
             claims[b, i * CAP : (i + 1) * CAP, :] = one_hot(
                 asked_by[b, 0:CAP, i : i + 1].astype(I32) == row_lane
             )
-
-        @pl.when(b == 1)
-        def _():
-            pass_sums(1)
 
         return carry
 
@@ -566,7 +522,7 @@
     hidden = jnp.maximum(hidden + vec[2:3, 0:EMB], 0.0).astype(BF16)
     embedding[...] = (mm(hidden, w_out[...]) + vec[3:4, 0:EMB]).T.astype(BF16)
 
-    for dy in (2, 0, 1, 3):
+    for dy in (2, 1, 3, 0):
         first = 1 if dy == 0 else 0
         wait_bytes(main_recv.at[dy, first:32], recv_main.at[dy])
         wait_bytes(ext_recv.at[dy, first:32], recv_ext.at[dy])
@@ -613,13 +569,10 @@
     wait_bytes(w_all.at[0:3, 0:544], send_sem.at[2])
     wait_bytes(wx_all.at[0:3], send_sem.at[3])
     wait_bytes(row_send.at[0:31], send_sem.at[4])
-    wait_bytes(relay_rows, send_sem.at[4])
     wait_bytes(main_recv.at[0:3], send_sem.at[5])
     wait_bytes(main_recv.at[3, 0:31], send_sem.at[5])
-    wait_bytes(relay_main, send_sem.at[5])
     wait_bytes(ext_recv.at[0:3], send_sem.at[6])
     wait_bytes(ext_recv.at[3, 0:31], send_sem.at[6])
-    wait_bytes(relay_ext, send_sem.at[6])
 
 
 def step(
@@ -688,9 +641,6 @@
             V((4, 32, CAP, 128), BF16),
             V((4, 4, 8, 1, 128), F32),
             V((4, 32, 1, 128), F32),
-            V((6, CAP, 256), BF16),
-            V((26, CAP, 128), BF16),
-            V((26, 1, 128), F32),
             V((8, 256), F32),
             V((256, ROWS), F32),
             V((ROWS, 256), BF16),
@@ -712,7 +662,7 @@
             V((16, 384), F32),
             V((EV, 384), F32),
             V((4, K * 128, SLOTS), BF16),
-            V((K, 128, 256), F32),
+            V((4, K, 128, 256), F32),
             V((2, EV, 384), F32),
             V((4, SLOTS, ROWS), BF16),
             V((4, 128, 128), F32),
@@ -721,11 +671,10 @@
             V((144, ROWS), F32),
             D((7,)),
             D((6,)),
-            D,
+            D((4,)),
             D((3,)),
             D((4,)),
             D((4,)),
-            D((5,)),
             D((19,)),
         ]
         + [V(a.shape, a.dtype) for a in args],

time: 77.2 us -> 61.9 us (0.80)
  the two profiles are of different devices: /device:TPU:6 before, /device:TPU:1 now
where the time goes in v4:
time: 61.9 us; the launch traced here: 60.9 us
  Pallas kernels  57.9 us (94%)
  local copies, waits for them, and re-layouts  2.33 us (4%)
  between operations  0.66 us (1%)
    pallas_call x1, Pallas kernels, step(): pl.pallas_call(kernel, out_shape=(jax.ShapeDtypeStruct((EMB, EV), BF16),...  57.9 us
    unnamed x4, local copies, waits for them, and re-layouts  2.33 us

profile of v4, /device:TPU:1, one launch (start us, length us, event | category | flops | bytes accessed | tf_op | source)
XLA Modules:
  0.0 60.9 jit_solution(9083077780089883651)
XLA Ops:
  0.6 57.9 %shard_map.194 = (bf16[172,512]{1,0:T(8,128)(2,1)}, f32[43,1024]{1,0:T(8,128)}) custom-call(f32[172,1024]{1,0:T(8,128)} %bitcast.15, s32[1,1024]{1,0:T(1,128)} %bitcast.24, s32[1,512]{1,0:T(1,128)} %bitcast.25, s32[10,512]{1,0:T(8,128)} %bitcast.22, s32[1,1536]{1,0:T(1,128)} %refs_4_.1, s32[12,512]{1,0:T(8,128)} %bitcast.23, bf16[64,2048]{1,0:T(8,128)(2,1)} %bitcast.17, ...), custom_call_target="tpu_custom_call" | custom-call | tf_op jit(solution)/shard_map/pallas_call | solution.py:622
  58.6 0.0 copy-start
  58.6 1.6 %copy.23 = bf16[512,172]{0,1:T(8,128)(2,1)} copy(bf16[512,172]{0,1:T(8,128)(2,1)} %bitcast.19) | data formatting | bytes 352256
  60.2 0.0 copy-done
  60.2 0.7 %copy.24 = f32[1024,43]{0,1:T(8,128)} copy(f32[1024,43]{0,1:T(8,128)S(1)} %bitcast.18) | data formatting | bytes 352256
Async XLA Ops:
  58.6 1.7 %copy-start = (f32[43,1024]{1,0:T(8,128)S(1)}, f32[43,1024]{1,0:T(8,128)}, u32[]{:S(2)}) copy-start(f32[43,1024]{1,0:T(8,128)} %get-tuple-element.5) | copy-start | bytes 528388

commit v5 on v4

--- a/solution.py
+++ b/solution.py
@@ -87,7 +87,6 @@
         zed,
         own,
         end_cols,
-        hits,
         ends,
         src,
         msg,
@@ -140,10 +139,8 @@
     at_z = [((z + d) % 4) * 2 for d in range(4)]
     at_c = [(c + d) % 2 for d in range(2)]
     at_f = [(f + d) % 4 for d in range(4)]
-    in_y = [at_z[j // 2] + at_c[j % 2] for j in range(8)]
-
-    def peer(dy, j, dx):
-        return at_y[dy] + in_y[j], at_f[dx]
+    def peer(t, i, dx):
+        return at_y[i // 2] + at_z[(t - i // 2) % 4] + at_c[i % 2], at_f[dx]
 
     def send(src_ref, dst_ref, s_sem, r_sem, to):
         pltpu.make_async_remote_copy(
@@ -158,17 +155,17 @@
     def wait_bytes(ref, sem):
         pltpu.make_async_copy(ref, ref, sem).wait()
 
-    everyone = [(dy, dx, j) for dy in range(4) for dx in range(4) for j in range(8)][1:]
+    everyone = [(t, dx, i) for t in range(4) for dx in range(4) for i in range(8)][1:]
 
     for dx in range(4):
         w_all[dx, 176:256, :] = jnp.zeros((80, 128), BF16)
         w_all[dx, 368:384, :] = jnp.zeros((16, 128), BF16)
 
     barrier = pltpu.get_barrier_semaphore()
-    near_by = [(dy, dx, j) for dy, dx, j in everyone if dx == 0 or (dy == 0 and j == 0)]
-    for dy, dx, j in near_by:
+    near_by = [(t, dx, i) for t, dx, i in everyone if dx == 0 or (t == 0 and i == 0)]
+    for t, dx, i in near_by:
         pl.semaphore_signal(
-            barrier, inc=1, device_id=peer(dy, j, dx), device_id_type=MESH
+            barrier, inc=1, device_id=peer(t, i, dx), device_id_type=MESH
         )
     for first in (4, 0, 1, 6):
         loads[first].start()
@@ -197,14 +194,14 @@
 
     pl.semaphore_wait(barrier, len(near_by))
 
-    for dy, dx, j in everyone:
+    for t, dx, i in everyone:
         if dx == 0:
-            to = peer(dy, j, 0)
+            to = peer(t, i, 0)
             send(
                 req_send.at[to[0]],
-                req_recv.at[dy * 32 + j],
+                req_recv.at[t * 32 + i],
                 send_sem.at[0],
-                recv_req.at[2 + dy],
+                recv_req.at[2 + t],
                 to,
             )
     for dx in range(1, 4):
@@ -263,47 +260,46 @@
     for k in range(K):
         times[k] = cosine(cols[:, 16 + k : 17 + k] * freq + phase).astype(BF16).astype(F32)
 
-    for dy in range(4):
-        first = 1 if dy == 0 else 0
-        wait_bytes(req_recv.at[dy * 32 + first : dy * 32 + 8], recv_req.at[2 + dy])
+    for t in range(4):
+        first = 1 if t == 0 else 0
+        wait_bytes(req_recv.at[t * 32 + first : t * 32 + 8], recv_req.at[2 + t])
     small[...] = jnp.zeros(small.shape, F32)
-    for dy in range(4):
-        small[8 * dy : 8 * dy + 8, :] = req_recv[dy * 32 : dy * 32 + 8].reshape(8, 128).astype(F32)
+    for t in range(4):
+        small[8 * t : 8 * t + 8, :] = req_recv[t * 32 : t * 32 + 8].reshape(8, 128).astype(F32)
     asked = small[...].T.astype(I32)
     row_lane = iota((CAP, ROWS), 1)
-    for dy in (2, 1, 3, 0):
+    for t in (2, 1, 3, 0):
         mask = jnp.concatenate(
             [
-                one_hot(asked[0:CAP, 8 * dy + j : 8 * dy + j + 1] == row_lane)
-                for j in range(8)
+                one_hot(asked[0:CAP, 8 * t + i : 8 * t + i + 1] == row_lane)
+                for i in range(8)
             ],
             axis=0,
         )
         rows = mm(mask, memb[...]).astype(BF16)
-        for j in range(8):
-            if dy == 0 and j == 0:
+        for i in range(8):
+            if t == 0 and i == 0:
                 fetched[n] = rows[0:CAP, :]
             else:
-                row_send[dy * 8 + j] = rows[j * CAP : (j + 1) * CAP, :]
-        for j in (4, 5, 2, 3, 6, 7, 1, 0):
-            if dy == 0 and j == 0:
+                row_send[t * 8 + i] = rows[i * CAP : (i + 1) * CAP, :]
+        for i in (4, 2, 6, 0, 5, 3, 7, 1):
+            if t == 0 and i == 0:
                 continue
-            back = (4 - j // 2) % 4 * 2 + j % 2
             send(
-                row_send.at[dy * 8 + j],
+                row_send.at[t * 8 + i],
                 fetched.at[n],
                 send_sem.at[4],
-                recv_rows.at[dy],
-                peer((4 - dy) % 4, back, 0),
+                recv_rows,
+                peer((4 - t) % 4, (4 - i // 2) % 4 * 2 + i % 2, 0),
             )
 
     wait_bytes(edge_recv.at[0:3], recv_x.at[0])
-    for dy, dx, j in everyone:
+    for t, dx, i in everyone:
         if dx != 0:
-            to = peer(dy, j, dx)
+            to = peer(t, i, dx)
             send(
                 req_send.at[to[0]],
-                req_recv.at[dy * 32 + dx * 8 + j],
+                req_recv.at[t * 32 + dx * 8 + i],
                 send_sem.at[0],
                 recv_req.at[1],
                 to,
@@ -311,17 +307,16 @@
 
     slot_lane = iota((128, SLOTS), 1)
 
-    def mark(b, count):
-        picks = cols[pl.ds(pl.multiple_of(b * 128, 128), 128), :].astype(I32)
+    def mark(b, carry):
+        rows = pl.ds(pl.multiple_of(b * 128, 128), 128)
+        picks = cols[rows, :].astype(I32)
         for k in range(K):
             hot[b, k * 128 : (k + 1) * 128, :] = one_hot(picks[:, 2 + k : 3 + k] == slot_lane)
         for e in range(2):
-            mask = jnp.where(picks[:, e : e + 1] == slot_lane, 1.0, 0.0)
-            count += jnp.sum(mask, axis=0, keepdims=True)
-            ends[e, pl.ds(pl.multiple_of(b * 128, 128), 128), :] = mask.astype(BF16)
-        return count
-
-    hits[...] = lax.fori_loop(0, 4, mark, jnp.zeros((1, SLOTS), F32))
+            ends[e, rows, :] = one_hot(picks[:, e : e + 1] == slot_lane)
+        return carry
+
+    lax.fori_loop(0, 4, mark, 0)
 
     r272 = iota((384, ATT), 0)
     c272 = iota((384, ATT), 1)
@@ -367,38 +362,29 @@
         msg[e * EV : (e + 1) * EV, 384:640] = edges
     ext_send[...] = jnp.zeros(ext_send.shape, F32)
 
-    def half_of(table_of, lanes_of, half):
-        return (
-            jnp.concatenate([table_of(dy) for dy in half], axis=0),
-            lambda ref: jnp.concatenate([lanes_of(ref, dy) for dy in half], axis=1),
-        )
-
-    def owners(dy):
-        return fetched[pl.ds(at_y[dy], 8)].reshape(384, 256)
-
-    def marks(view, dy):
-        return view[:, pl.ds(pl.multiple_of(at_y[dy] * CAP, 128), 384)]
-
-    for dy in (1, 2):
-        wait_bytes(fetched.at[0:8], recv_rows.at[dy])
-    table, lanes = half_of(owners, marks, (1, 2))
+    wait_bytes(req_recv.at[0:96], recv_req.at[1])
+    for t in range(4):
+        small[...] = jnp.zeros(small.shape, F32)
+        small[0:32, :] = req_recv[t * 32 : t * 32 + 32].reshape(32, 128).astype(F32)
+        asked_by[t] = small[...].T
+
+    def claim(t, carry):
+        for i in range(32):
+            claims[t, i * CAP : (i + 1) * CAP, :] = one_hot(
+                asked_by[t, 0:CAP, i : i + 1].astype(I32) == row_lane
+            )
+        return carry
+
+    lax.fori_loop(0, 4, claim, 0)
+
+    wait_bytes(fetched.at[0:31], recv_rows)
+    table = fetched.reshape(SLOTS, 256)
     for e in range(2):
-        src[e] = mm(lanes(ends.at[e]), table)
-
-    def first_half(b, carry):
-        table, lanes = half_of(owners, marks, (1, 2))
-        near[b] = mm(lanes(hot.at[b]), table).reshape(K, 128, 256)
-        return carry
-
-    lax.fori_loop(0, 4, first_half, 0)
-
-    wait_bytes(fetched.at[0:8], recv_rows.at[3])
-    wait_bytes(fetched.at[0:7], recv_rows.at[0])
-    table, lanes = half_of(owners, marks, (3, 0))
+        src[e] = mm(ends[e], table[...])
+    lane = iota((EV, 256), 1)
+    counted = (lane == MEM + 2) | (lane == MEM + 3)
     for e in range(2):
-        src[e] += mm(lanes(ends.at[e]), table)
-    for e in range(2):
-        msg[e * EV : (e + 1) * EV, 0:256] = src[1 - e].astype(BF16)
+        msg[e * EV : (e + 1) * EV, 0:256] = jnp.where(counted, 1.0, src[1 - e]).astype(BF16)
         stamp = src[e, :, MEM : MEM + 1] * 128.0 + src[e, :, MEM + 1 : MEM + 2]
         gap = cols[:, 32:33] - stamp
         msg[e * EV : (e + 1) * EV, 256:384] = cosine(gap * freq + phase).astype(BF16)
@@ -406,45 +392,63 @@
     wait_bytes(w_all.at[0:3, 0:544], recv_x.at[1])
     wait_bytes(wx_all.at[0:3], recv_x.at[2])
     rows4 = jnp.concatenate([wx_all[dx] for dx in range(4)] + [jnp.zeros((4, 640), F32)], axis=0)
-    w_ext[...] = rows4.astype(BF16)
-
-    for dy in (2, 1, 3, 0):
-        base = at_y[dy] * CAP
-        mask = one_hot(iota((384, 2 * EV), 0) + base == end_cols[...])
-        sums = mm(mask, msg[...]).astype(BF16)
+    row = iota((8, 640), 0)
+    counts = (row >= 4) & (row < 6) & (iota((8, 640), 1) == row + (MEM + 2 - 4))
+    w_ext[...] = jnp.where(counts, 1.0, rows4).astype(BF16)
+
+    lane = iota((384, 256), 1)
+    for t in (2, 1, 3, 0):
+        mask = jnp.concatenate(
+            [
+                one_hot(
+                    iota((2 * CAP, 2 * EV), 0) + (at_y[dy] + at_z[(t - dy) % 4]) * CAP
+                    == end_cols[...]
+                )
+                for dy in range(4)
+            ],
+            axis=0,
+        )
+        total = mm(mask, msg[...])
+        first = total[:, 0:256]
+        high = jnp.floor(first * (1.0 / 128.0))
+        first = jnp.where(
+            lane == MEM + 2, first - high * 128.0, jnp.where(lane == MEM + 3, high, first)
+        )
+        sums = jnp.concatenate([first, total[:, 256:640]], axis=1).astype(BF16)
         for pair in range(2):
             w_pair = jnp.concatenate([w_all[2 * pair], w_all[2 * pair + 1]], axis=1)
             out = mm(sums, w_pair).astype(BF16)
             for i in range(2):
-                main_send[dy, 2 * pair + i] = out[:, i * 128 : (i + 1) * 128].reshape(8, CAP, 128)
+                main_send[t, 2 * pair + i] = out[:, i * 128 : (i + 1) * 128].reshape(8, CAP, 128)
         ext_tmp[0:8, :] = mm_nt(w_ext[...], sums)
-        ext_tmp[8:9, :] = hits[:, pl.ds(pl.multiple_of(base, 128), 384)]
+        ext_tmp[8:9, :] = ext_tmp[4:5, :] + ext_tmp[5:6, :] * 128.0
         for j in range(8):
             count_row = ext_tmp[8:9, j * CAP : (j + 1) * CAP]
             for dx in range(4):
-                ext_send[dy, dx, j, :, 0:CAP] = ext_tmp[dx : dx + 1, j * CAP : (j + 1) * CAP]
-                ext_send[dy, dx, j, :, 64 : 64 + CAP] = count_row
-        for j in range(8):
-            for dx in range(4):
-                if dy == 0 and dx == 0 and j == 0:
+                ext_send[t, dx, j, :, 0:CAP] = ext_tmp[dx : dx + 1, j * CAP : (j + 1) * CAP]
+                ext_send[t, dx, j, :, 64 : 64 + CAP] = count_row
+        for i in (4, 2, 6, 0, 5, 3, 7, 1):
+            for dx in (2, 1, 3, 0):
+                if t == 0 and dx == 0 and i == 0:
                     continue
-                to = peer(dy, j, dx)
+                to = peer(t, i, dx)
+                at = i // 2 * 2 + at_c[i % 2]
                 send(
-                    main_send.at[dy, dx, in_y[j]],
-                    main_recv.at[dy, dx * 8 + j],
+                    main_send.at[t, dx, at],
+                    main_recv.at[t, dx * 8 + i],
                     send_sem.at[5],
-                    recv_main.at[dy],
+                    recv_main.at[t],
                     to,
                 )
                 send(
-                    ext_send.at[dy, dx, in_y[j]],
-                    ext_recv.at[dy, dx * 8 + j],
+                    ext_send.at[t, dx, at],
+                    ext_recv.at[t, dx * 8 + i],
                     send_sem.at[6],
-                    recv_ext.at[dy],
+                    recv_ext.at[t],
                     to,
                 )
-    main_recv[0, 0] = main_send[0, 0, in_y[0]]
-    ext_recv[0, 0] = ext_send[0, 0, in_y[0]]
+    main_recv[0, 0] = main_send[0, 0, at_c[0]]
+    ext_recv[0, 0] = ext_send[0, 0, at_c[0]]
 
     still = jnp.broadcast_to(cosine(phase), (EV, 128)).astype(BF16)
     query[...] = (
@@ -458,16 +462,9 @@
         fine = (part - coarse.astype(F32)).astype(BF16)
         qk[h] = mm_nt(coarse, wkv[:, 0:384]) + mm_nt(fine, wkv[:, 0:384])
 
-    wait_bytes(req_recv.at[0:96], recv_req.at[1])
-    for dy in range(4):
-        small[...] = jnp.zeros(small.shape, F32)
-        small[0:32, :] = req_recv[dy * 32 : dy * 32 + 32].reshape(32, 128).astype(F32)
-        asked_by[dy] = small[...].T
-
     def attend(b, carry):
         at = pl.multiple_of(b * 128, 128)
-        table, lanes = half_of(owners, marks, (3, 0))
-        near[b] += mm(lanes(hot.at[b]), table).reshape(K, 128, 256)
+        near[...] = mm(hot[b], table[...]).reshape(K, 128, 256)
 
         def group(g, inner):
             r = pl.multiple_of(g * 16, 16)
@@ -475,7 +472,7 @@
             q0, q1 = qk[0, rows, :], qk[1, rows, :]
             s0, s1 = [], []
             for k in range(K):
-                x, t = near[b, k, pl.ds(r, 16), :], times[k, rows, :]
+                x, t = near[k, pl.ds(r, 16), :], times[k, rows, :]
                 u0 = x * q0[:, 0:256]
                 u1 = x * q1[:, 0:256]
                 u0 = u0[:, 0:128] + u0[:, 128:256] + t * q0[:, 256:384]
@@ -491,7 +488,7 @@
             a0 = a1 = jnp.zeros((16, 256), F32)
             c0 = c1 = jnp.zeros((16, 128), F32)
             for k in range(K):
-                x, t = near[b, k, pl.ds(r, 16), :], times[k, rows, :]
+                x, t = near[k, pl.ds(r, 16), :], times[k, rows, :]
                 a0 += p0[k] * x
                 a1 += p1[k] * x
                 c0 += p0[k] * t
@@ -503,11 +500,6 @@
             return inner
 
         lax.fori_loop(0, 8, group, 0, unroll=2)
-        for i in range(32):
-            claims[b, i * CAP : (i + 1) * CAP, :] = one_hot(
-                asked_by[b, 0:CAP, i : i + 1].astype(I32) == row_lane
-            )
-
         return carry
 
     lax.fori_loop(0, 4, attend, 0)
@@ -522,13 +514,13 @@
     hidden = jnp.maximum(hidden + vec[2:3, 0:EMB], 0.0).astype(BF16)
     embedding[...] = (mm(hidden, w_out[...]) + vec[3:4, 0:EMB]).T.astype(BF16)
 
-    for dy in (2, 1, 3, 0):
-        first = 1 if dy == 0 else 0
-        wait_bytes(main_recv.at[dy, first:32], recv_main.at[dy])
-        wait_bytes(ext_recv.at[dy, first:32], recv_ext.at[dy])
+    for t in (2, 1, 3, 0):
+        first = 1 if t == 0 else 0
+        wait_bytes(main_recv.at[t, first:32], recv_main.at[t])
+        wait_bytes(ext_recv.at[t, first:32], recv_ext.at[t])
         for i in range(32):
-            side[0:1, i * CAP : (i + 1) * CAP] = ext_recv[dy, i, :, 0:CAP]
-            side[1:2, i * CAP : (i + 1) * CAP] = ext_recv[dy, i, :, 64 : 64 + CAP]
+            side[0:1, i * CAP : (i + 1) * CAP] = ext_recv[t, i, :, 0:CAP]
+            side[1:2, i * CAP : (i + 1) * CAP] = ext_recv[t, i, :, 64 : 64 + CAP]
         count = side[1:2, :]
         high = jnp.floor(count * (1.0 / 128.0))
         row = iota((16, SLOTS), 0)
@@ -538,10 +530,10 @@
             jnp.where(row == 1, count - high * 128.0, jnp.where(row == 2, high, 0.0)),
         )
         left = jnp.concatenate(
-            [main_recv[dy].reshape(SLOTS, 128).T, rest.astype(BF16)], axis=0
+            [main_recv[t].reshape(SLOTS, 128).T, rest.astype(BF16)], axis=0
         )
-        total = mm(left, claims[dy])
-        if dy == 2:
+        total = mm(left, claims[t])
+        if t == 2:
             acc[...] = total
         else:
             acc[...] += total
@@ -655,14 +647,13 @@
             V((4, CAP, ROWS), F32),
             V((CAP, ROWS), F32),
             V((1, 2 * EV), I32),
-            V((1, SLOTS), F32),
             V((2, EV, SLOTS), BF16),
             V((2, EV, 256), F32),
             V((2 * EV, 640), BF16),
             V((16, 384), F32),
             V((EV, 384), F32),
             V((4, K * 128, SLOTS), BF16),
-            V((4, K, 128, 256), F32),
+            V((K, 128, 256), F32),
             V((2, EV, 384), F32),
             V((4, SLOTS, ROWS), BF16),
             V((4, 128, 128), F32),
@@ -671,7 +662,7 @@
             V((144, ROWS), F32),
             D((7,)),
             D((6,)),
-            D((4,)),
+            D,
             D((3,)),
             D((4,)),
             D((4,)),

time: 61.9 us -> 57.5 us (0.929)
  Pallas kernels: 57.9 us -> 53.9 us
    pallas_call x1, Pallas kernels: 57.9 us -> 53.9 us  [step(): pl.pallas_call(kernel, out_shape=(jax.ShapeDtypeStruct((EMB, EV), BF16),...]
where the time goes in v5:
time: 57.5 us; the launch traced here: 56.8 us
  Pallas kernels  53.9 us (94%)
  local copies, waits for them, and re-layouts  2.33 us (4%)
  between operations  0.66 us (1%)
    pallas_call x1, Pallas kernels, step(): pl.pallas_call(kernel, out_shape=(jax.ShapeDtypeStruct((EMB, EV), BF16),...  53.9 us
    unnamed x4, local copies, waits for them, and re-layouts  2.33 us

profile of v5, /device:TPU:1, one launch (start us, length us, event | category | flops | bytes accessed | tf_op | source)
XLA Modules:
  0.0 56.8 jit_solution(14261028899571406864)
XLA Ops:
  0.6 53.9 %shard_map.194 = (bf16[172,512]{1,0:T(8,128)(2,1)}, f32[43,1024]{1,0:T(8,128)}) custom-call(f32[172,1024]{1,0:T(8,128)} %bitcast.15, s32[1,1024]{1,0:T(1,128)} %bitcast.24, s32[1,512]{1,0:T(1,128)} %bitcast.25, s32[10,512]{1,0:T(8,128)} %bitcast.22, s32[1,1536]{1,0:T(1,128)} %refs_4_.1, s32[12,512]{1,0:T(8,128)} %bitcast.23, bf16[64,2048]{1,0:T(8,128)(2,1)} %bitcast.17, ...), custom_call_target="tpu_custom_call" | custom-call | tf_op jit(solution)/shard_map/pallas_call | solution.py:614
  54.5 0.0 copy-start
  54.5 1.6 %copy.23 = bf16[512,172]{0,1:T(8,128)(2,1)} copy(bf16[512,172]{0,1:T(8,128)(2,1)} %bitcast.19) | data formatting | bytes 352256
  56.2 0.0 copy-done
  56.2 0.7 %copy.24 = f32[1024,43]{0,1:T(8,128)} copy(f32[1024,43]{0,1:T(8,128)S(1)} %bitcast.18) | data formatting | bytes 352256
Async XLA Ops:
  54.5 1.7 %copy-start = (f32[43,1024]{1,0:T(8,128)S(1)}, f32[43,1024]{1,0:T(8,128)}, u32[]{:S(2)}) copy-start(f32[43,1024]{1,0:T(8,128)} %get-tuple-element.5) | copy-start | bytes 528388

commit v6 on v5

--- a/solution.py
+++ b/solution.py
@@ -238,28 +238,6 @@
     w_all[0] = w_mine[...]
     wx_all[0] = wx_mine[...]
 
-    for i in (2, 3, 5, 7, 8, 9, 10, 11, 12, 13, 14, 15, 17, 18):
-        loads[i].wait()
-    vec[...] = jnp.zeros(vec.shape, F32)
-    vec[0:1, 0:TIME] = frequency[...]
-    vec[1:2, 0:TIME] = phase_shift[...]
-    vec[2:3, 0:EMB] = b_merge[...]
-    vec[3:4, 0:EMB] = b_out[...]
-    vec[4:8, 0:UNITS] = gru_bias[...]
-    freq = vec[0:1, 0:128]
-    phase = vec[1:2, 0:128]
-
-    wide_t[...] = jnp.zeros(wide_t.shape, F32)
-    wide_t[0 : K + 2, :] = slot_ref[...].astype(F32)
-    wide_t[16 : 16 + K, :] = nbr_gap[...].astype(F32)
-    wide_t[32:33, :] = ev_time[...].astype(F32)
-    cols[...] = wide_t[...].T
-    end_cols[:, 0:EV] = slot_ref[0:1, :]
-    end_cols[:, EV : 2 * EV] = slot_ref[1:2, :]
-
-    for k in range(K):
-        times[k] = cosine(cols[:, 16 + k : 17 + k] * freq + phase).astype(BF16).astype(F32)
-
     for t in range(4):
         first = 1 if t == 0 else 0
         wait_bytes(req_recv.at[t * 32 + first : t * 32 + 8], recv_req.at[2 + t])
@@ -305,6 +283,28 @@
                 to,
             )
 
+    for i in (2, 3, 5, 7, 8, 9, 10, 11, 12, 13, 14, 15, 17, 18):
+        loads[i].wait()
+    vec[...] = jnp.zeros(vec.shape, F32)
+    vec[0:1, 0:TIME] = frequency[...]
+    vec[1:2, 0:TIME] = phase_shift[...]
+    vec[2:3, 0:EMB] = b_merge[...]
+    vec[3:4, 0:EMB] = b_out[...]
+    vec[4:8, 0:UNITS] = gru_bias[...]
+    freq = vec[0:1, 0:128]
+    phase = vec[1:2, 0:128]
+
+    wide_t[...] = jnp.zeros(wide_t.shape, F32)
+    wide_t[0 : K + 2, :] = slot_ref[...].astype(F32)
+    wide_t[16 : 16 + K, :] = nbr_gap[...].astype(F32)
+    wide_t[32:33, :] = ev_time[...].astype(F32)
+    cols[...] = wide_t[...].T
+    end_cols[:, 0:EV] = slot_ref[0:1, :]
+    end_cols[:, EV : 2 * EV] = slot_ref[1:2, :]
+
+    for k in range(K):
+        times[k] = cosine(cols[:, 16 + k : 17 + k] * freq + phase).astype(BF16).astype(F32)
+
     slot_lane = iota((128, SLOTS), 1)
 
     def mark(b, carry):
@@ -415,11 +415,24 @@
             lane == MEM + 2, first - high * 128.0, jnp.where(lane == MEM + 3, high, first)
         )
         sums = jnp.concatenate([first, total[:, 256:640]], axis=1).astype(BF16)
-        for pair in range(2):
+        for pair in (1, 0):
             w_pair = jnp.concatenate([w_all[2 * pair], w_all[2 * pair + 1]], axis=1)
             out = mm(sums, w_pair).astype(BF16)
-            for i in range(2):
-                main_send[t, 2 * pair + i] = out[:, i * 128 : (i + 1) * 128].reshape(8, CAP, 128)
+            for half in range(2):
+                main_send[t, 2 * pair + half] = out[:, half * 128 : (half + 1) * 128].reshape(
+                    8, CAP, 128
+                )
+            for i in (4, 2, 6, 0, 5, 3, 7, 1):
+                for dx in (2 * pair, 2 * pair + 1):
+                    if t == 0 and dx == 0 and i == 0:
+                        continue
+                    send(
+                        main_send.at[t, dx, i // 2 * 2 + at_c[i % 2]],
+                        main_recv.at[t, dx * 8 + i],
+                        send_sem.at[5],
+                        recv_main.at[t],
+                        peer(t, i, dx),
+                    )
         ext_tmp[0:8, :] = mm_nt(w_ext[...], sums)
         ext_tmp[8:9, :] = ext_tmp[4:5, :] + ext_tmp[5:6, :] * 128.0
         for j in range(8):
@@ -428,24 +441,15 @@
                 ext_send[t, dx, j, :, 0:CAP] = ext_tmp[dx : dx + 1, j * CAP : (j + 1) * CAP]
                 ext_send[t, dx, j, :, 64 : 64 + CAP] = count_row
         for i in (4, 2, 6, 0, 5, 3, 7, 1):
-            for dx in (2, 1, 3, 0):
+            for dx in (2, 3, 1, 0):
                 if t == 0 and dx == 0 and i == 0:
                     continue
-                to = peer(t, i, dx)
-                at = i // 2 * 2 + at_c[i % 2]
                 send(
-                    main_send.at[t, dx, at],
-                    main_recv.at[t, dx * 8 + i],
-                    send_sem.at[5],
-                    recv_main.at[t],
-                    to,
-                )
-                send(
-                    ext_send.at[t, dx, at],
+                    ext_send.at[t, dx, i // 2 * 2 + at_c[i % 2]],
                     ext_recv.at[t, dx * 8 + i],
                     send_sem.at[6],
                     recv_ext.at[t],
-                    to,
+                    peer(t, i, dx),
                 )
     main_recv[0, 0] = main_send[0, 0, at_c[0]]
     ext_recv[0, 0] = ext_send[0, 0, at_c[0]]
@@ -512,7 +516,7 @@
     attended = jnp.where(head_of, halves[0], halves[1]).astype(BF16)
     hidden = mm(attended, wm[0:384, :]) + mm(src[0].astype(BF16), wm[384:640, :])
     hidden = jnp.maximum(hidden + vec[2:3, 0:EMB], 0.0).astype(BF16)
-    embedding[...] = (mm(hidden, w_out[...]) + vec[3:4, 0:EMB]).T.astype(BF16)
+    embedding[...] = (mm(hidden, w_out[...]) + vec[3:4, 0:EMB]).T
 
     for t in (2, 1, 3, 0):
         first = 1 if t == 0 else 0
@@ -614,7 +618,7 @@
     embedding, new_memory = pl.pallas_call(
         kernel,
         out_shape=(
-            jax.ShapeDtypeStruct((EMB, EV), BF16),
+            jax.ShapeDtypeStruct((EMB, EV), F32),
             jax.ShapeDtypeStruct((UNITS, ROWS), F32),
         ),
         in_specs=[pl.BlockSpec(memory_space=pl.ANY)] * len(args),
@@ -673,7 +677,7 @@
             collective_id=0, has_side_effects=True, vmem_limit_bytes=60 * 1024 * 1024
         ),
     )(*args)
-    return embedding.T, new_memory.T
+    return embedding.T.astype(BF16), new_memory.T
 
 
 def solution(mesh):

time: 57.5 us -> 62 us (1.078)
  the two profiles are of different devices: /device:TPU:1 before, /device:TPU:0 now
where the time goes in v6:
time: 62 us; the launch traced here: 61.8 us
  Pallas kernels  58.8 us (95%)
  other arithmetic  1.72 us (3%)
  local copies, waits for them, and re-layouts  0.68 us (1%)
  between operations  0.66 us (1%)
    pallas_call x1, Pallas kernels, step(): pl.pallas_call(kernel, out_shape=(jax.ShapeDtypeStruct((EMB, EV), F32), j...  58.8 us
    convert_element_type x1, other arithmetic, step(): return (embedding.T.astype(BF16), new_memory.T)  1.72 us

profile of v6, /device:TPU:0, one launch (start us, length us, event | category | flops | bytes accessed | tf_op | source)
XLA Modules:
  0.0 61.8 jit_solution(16527954014838438844)
XLA Ops:
  0.6 58.8 %shard_map.194 = (f32[172,512]{1,0:T(8,128)}, f32[43,1024]{1,0:T(8,128)}) custom-call(f32[172,1024]{1,0:T(8,128)} %bitcast.16, s32[1,1024]{1,0:T(1,128)} %bitcast.24, s32[1,512]{1,0:T(1,128)} %bitcast.25, s32[10,512]{1,0:T(8,128)} %bitcast.22, s32[1,1536]{1,0:T(1,128)} %refs_4_.1, s32[12,512]{1,0:T(8,128)} %bitcast.23, bf16[64,2048]{1,0:T(8,128)(2,1)} %bitcast.18, ...), custom_call_target="tpu_custom_call" | custom-call | tf_op jit(solution)/shard_map/pallas_call | solution.py:618
  59.4 0.0 copy-start
  59.4 1.7 %convert_bitcast_fusion = bf16[512,172]{0,1:T(8,128)(2,1)} fusion(f32[172,512]{1,0:T(8,128)} %get-tuple-element.4), kind=kLoop, calls=%fused_computation | loop fusion | flops 88064 | bytes 528384 | tf_op jit(solution)/shard_map/convert_element_type | solution.py:680
  61.1 0.0 copy-done
  61.1 0.7 %copy.22 = f32[1024,43]{0,1:T(8,128)} copy(f32[1024,43]{0,1:T(8,128)S(1)} %bitcast.19) | data formatting | bytes 352256
Async XLA Ops:
  59.4 1.7 %copy-start = (f32[43,1024]{1,0:T(8,128)S(1)}, f32[43,1024]{1,0:T(8,128)}, u32[]{:S(2)}) copy-start(f32[43,1024]{1,0:T(8,128)} %get-tuple-element.5) | copy-start | bytes 528388

commit v7 on v5

--- a/solution.py
+++ b/solution.py
@@ -97,6 +97,7 @@
         qk,
         claims,
         asked_by,
+        bias,
         mix,
         side,
         acc,
@@ -260,6 +261,45 @@
     for k in range(K):
         times[k] = cosine(cols[:, 16 + k : 17 + k] * freq + phase).astype(BF16).astype(F32)
 
+    r272 = iota((384, ATT), 0)
+    c272 = iota((384, ATT), 1)
+    place = one_hot(
+        ((c272 < MEM) & (r272 == c272)) | ((c272 >= MEM) & (r272 == c272 + (256 - MEM)))
+    )
+    wkv[...] = jnp.zeros(wkv.shape, BF16)
+    wkv[:, 0:ATT] = mm(place, w_key[...]).astype(BF16)
+    wkv[:, 384 : 384 + ATT] = mm(place, w_value[...]).astype(BF16)
+    wq[...] = jnp.zeros(wq.shape, BF16)
+    wq[:, 0:ATT] = mm(place, w_query[...]).astype(BF16)
+    r444 = iota((640, ATT + MEM), 0)
+    c444 = iota((640, ATT + MEM), 1)
+    place = one_hot(
+        ((c444 < ATT) & (r444 == c444)) | ((c444 >= ATT) & (r444 == c444 + (384 - ATT)))
+    )
+    wm[...] = mm_nt(place, w_merge[...]).astype(BF16)
+
+    widen = one_hot(iota((CAP, UNITS), 0) == iota((CAP, UNITS), 1))
+    mem_b = memory[...].astype(BF16)
+    gates = (
+        w_input[0, :, 0:MEM] + w_hidden[0],
+        w_input[1, :, 0:MEM] + w_hidden[1],
+        w_input[2, :, 0:MEM],
+        w_hidden[2],
+    )
+    for g, w in enumerate(gates):
+        zed[g] = mm(mm(widen, w.astype(BF16)).astype(BF16), mem_b)
+    own[...] = jnp.dot(
+        jnp.where(
+            (iota((CAP, MEM), 1) == iota((CAP, MEM), 0) + f * UNITS)
+            & (iota((CAP, MEM), 0) < UNITS),
+            1.0,
+            0.0,
+        ),
+        memory[...],
+        preferred_element_type=F32,
+        precision=lax.Precision.HIGHEST,
+    )
+
     for t in range(4):
         first = 1 if t == 0 else 0
         wait_bytes(req_recv.at[t * 32 + first : t * 32 + 8], recv_req.at[2 + t])
@@ -318,51 +358,15 @@
 
     lax.fori_loop(0, 4, mark, 0)
 
-    r272 = iota((384, ATT), 0)
-    c272 = iota((384, ATT), 1)
-    place = one_hot(
-        ((c272 < MEM) & (r272 == c272)) | ((c272 >= MEM) & (r272 == c272 + (256 - MEM)))
-    )
-    wkv[...] = jnp.zeros(wkv.shape, BF16)
-    wkv[:, 0:ATT] = mm(place, w_key[...]).astype(BF16)
-    wkv[:, 384 : 384 + ATT] = mm(place, w_value[...]).astype(BF16)
-    wq[...] = jnp.zeros(wq.shape, BF16)
-    wq[:, 0:ATT] = mm(place, w_query[...]).astype(BF16)
-    r444 = iota((640, ATT + MEM), 0)
-    c444 = iota((640, ATT + MEM), 1)
-    place = one_hot(
-        ((c444 < ATT) & (r444 == c444)) | ((c444 >= ATT) & (r444 == c444 + (384 - ATT)))
-    )
-    wm[...] = mm_nt(place, w_merge[...]).astype(BF16)
-
-    widen = one_hot(iota((CAP, UNITS), 0) == iota((CAP, UNITS), 1))
-    mem_b = memory[...].astype(BF16)
-    gates = (
-        w_input[0, :, 0:MEM] + w_hidden[0],
-        w_input[1, :, 0:MEM] + w_hidden[1],
-        w_input[2, :, 0:MEM],
-        w_hidden[2],
-    )
-    for g, w in enumerate(gates):
-        zed[g] = mm(mm(widen, w.astype(BF16)).astype(BF16), mem_b)
-    own[...] = jnp.dot(
-        jnp.where(
-            (iota((CAP, MEM), 1) == iota((CAP, MEM), 0) + f * UNITS)
-            & (iota((CAP, MEM), 0) < UNITS),
-            1.0,
-            0.0,
-        ),
-        memory[...],
-        preferred_element_type=F32,
-        precision=lax.Precision.HIGHEST,
-    )
-
     edges = edge_recv[...].reshape(256, EV).astype(F32).T.astype(BF16)
     for e in range(2):
         msg[e * EV : (e + 1) * EV, 384:640] = edges
     ext_send[...] = jnp.zeros(ext_send.shape, F32)
 
     wait_bytes(req_recv.at[0:96], recv_req.at[1])
+    small[...] = jnp.zeros(small.shape, F32)
+    small[0:4, :] = vec[4:8, 0:128]
+    bias[...] = small[...].T
     for t in range(4):
         small[...] = jnp.zeros(small.shape, F32)
         small[0:32, :] = req_recv[t * 32 : t * 32 + 32].reshape(32, 128).astype(F32)
@@ -499,7 +503,7 @@
             mix[1, rows, 256:384] = c1 * n1
             return inner
 
-        lax.fori_loop(0, 8, group, 0, unroll=2)
+        lax.fori_loop(0, 8, group, 0, unroll=4)
         return carry
 
     lax.fori_loop(0, 4, attend, 0)
@@ -538,9 +542,6 @@
         else:
             acc[...] += total
 
-    small[...] = jnp.zeros(small.shape, F32)
-    small[0:4, :] = vec[4:8, 0:128]
-    bias = small[...].T
     b0, b1, b2, b3 = (bias[0:UNITS, g : g + 1] for g in range(4))
     heard = acc[129:130, :] + acc[130:131, :] * 128.0
     share = 1.0 / jnp.maximum(heard, 1.0)
@@ -657,6 +658,7 @@
             V((2, EV, 384), F32),
             V((4, SLOTS, ROWS), BF16),
             V((4, 128, 128), F32),
+            V((128, 128), F32),
             V((2, EV, 384), F32),
             V((8, SLOTS), F32),
             V((144, ROWS), F32),

time: 57.5 us -> 56.8 us (0.988)
  no operation moved by 1% of the time
where the time goes in v7:
time: 56.8 us; the launch traced here: 56.7 us
  Pallas kernels  53.7 us (95%)
  local copies, waits for them, and re-layouts  2.33 us (4%)
  between operations  0.66 us (1%)
    pallas_call x1, Pallas kernels, step(): pl.pallas_call(kernel, out_shape=(jax.ShapeDtypeStruct((EMB, EV), BF16),...  53.7 us
    unnamed x4, local copies, waits for them, and re-layouts  2.33 us

profile of v7, /device:TPU:1, one launch (start us, length us, event | category | flops | bytes accessed | tf_op | source)
XLA Modules:
  0.0 56.7 jit_solution(6041271054496289861)
XLA Ops:
  0.6 53.7 %shard_map.194 = (bf16[172,512]{1,0:T(8,128)(2,1)}, f32[43,1024]{1,0:T(8,128)}) custom-call(f32[172,1024]{1,0:T(8,128)} %bitcast.15, s32[1,1024]{1,0:T(1,128)} %bitcast.24, s32[1,512]{1,0:T(1,128)} %bitcast.25, s32[10,512]{1,0:T(8,128)} %bitcast.22, s32[1,1536]{1,0:T(1,128)} %refs_4_.1, s32[12,512]{1,0:T(8,128)} %bitcast.23, bf16[64,2048]{1,0:T(8,128)(2,1)} %bitcast.17, ...), custom_call_target="tpu_custom_call" | custom-call | tf_op jit(solution)/shard_map/pallas_call | solution.py:615
  54.3 0.0 copy-start
  54.4 1.6 %copy.23 = bf16[512,172]{0,1:T(8,128)(2,1)} copy(bf16[512,172]{0,1:T(8,128)(2,1)} %bitcast.19) | data formatting | bytes 352256
  56.0 0.0 copy-done
  56.0 0.7 %copy.24 = f32[1024,43]{0,1:T(8,128)} copy(f32[1024,43]{0,1:T(8,128)S(1)} %bitcast.18) | data formatting | bytes 352256
Async XLA Ops:
  54.3 1.7 %copy-start = (f32[43,1024]{1,0:T(8,128)S(1)}, f32[43,1024]{1,0:T(8,128)}, u32[]{:S(2)}) copy-start(f32[43,1024]{1,0:T(8,128)} %get-tuple-element.5) | copy-start | bytes 528388

commit v8 on v7

--- a/solution.py
+++ b/solution.py
@@ -157,6 +157,12 @@
         pltpu.make_async_copy(ref, ref, sem).wait()
 
     everyone = [(t, dx, i) for t in range(4) for dx in range(4) for i in range(8)][1:]
+
+    def hops(pair):
+        t, dx, i = pair
+        return sum(min(d, 4 - d) for d in (i // 2, (t - i // 2) % 4, dx))
+
+    everyone.sort(key=hops, reverse=True)
 
     for dx in range(4):
         w_all[dx, 176:256, :] = jnp.zeros((80, 128), BF16)

time: 56.8 us -> 56.6 us (level)
  no operation moved by 1% of the time
where the time goes in v8:
time: 56.6 us; the launch traced here: 56.5 us
  Pallas kernels  53.5 us (95%)
  local copies, waits for them, and re-layouts  2.33 us (4%)
  between operations  0.66 us (1%)
    pallas_call x1, Pallas kernels, step(): pl.pallas_call(kernel, out_shape=(jax.ShapeDtypeStruct((EMB, EV), BF16),...  53.5 us
    unnamed x4, local copies, waits for them, and re-layouts  2.33 us

profile of v8, /device:TPU:1, one launch (start us, length us, event | category | flops | bytes accessed | tf_op | source)
XLA Modules:
  0.0 56.5 jit_solution(16814845432304856210)
XLA Ops:
  0.6 53.5 %shard_map.194 = (bf16[172,512]{1,0:T(8,128)(2,1)}, f32[43,1024]{1,0:T(8,128)}) custom-call(f32[172,1024]{1,0:T(8,128)} %bitcast.15, s32[1,1024]{1,0:T(1,128)} %bitcast.24, s32[1,512]{1,0:T(1,128)} %bitcast.25, s32[10,512]{1,0:T(8,128)} %bitcast.22, s32[1,1536]{1,0:T(1,128)} %refs_4_.1, s32[12,512]{1,0:T(8,128)} %bitcast.23, bf16[64,2048]{1,0:T(8,128)(2,1)} %bitcast.17, ...), custom_call_target="tpu_custom_call" | custom-call | tf_op jit(solution)/shard_map/pallas_call | solution.py:621
  54.1 0.0 copy-start
  54.1 1.6 %copy.23 = bf16[512,172]{0,1:T(8,128)(2,1)} copy(bf16[512,172]{0,1:T(8,128)(2,1)} %bitcast.19) | data formatting | bytes 352256
  55.8 0.0 copy-done
  55.8 0.7 %copy.24 = f32[1024,43]{0,1:T(8,128)} copy(f32[1024,43]{0,1:T(8,128)S(1)} %bitcast.18) | data formatting | bytes 352256
Async XLA Ops:
  54.1 1.7 %copy-start = (f32[43,1024]{1,0:T(8,128)S(1)}, f32[43,1024]{1,0:T(8,128)}, u32[]{:S(2)}) copy-start(f32[43,1024]{1,0:T(8,128)} %get-tuple-element.5) | copy-start | bytes 528388
